TPU v7x, 128 devices: a whole 4x4x4 slice. The times are simulated.
128 devices in a mesh: wide: 16 (over x, z), narrow: 8 (over y, core).
Axes of the slice: x: 4, y: 4, z: 4, core: 2. Of those that a mesh axis runs over, the one named last changes fastest.
Arguments:
- positions: float32 [3, 16384], P(None, ('wide', 'narrow')), may hold values from -1 to 69, as said below
- noise: float32 [3, 16, 16384], P(None, None, ('wide', 'narrow')), may hold values from -6 to 6
Outputs:
- displacement: float32 [3, 16, 16384], P(None, None, ('wide', 'narrow'))
Inputs may be any that keep to these rules, and one draw needn't show every extreme that they name: `positions`: any two particles lie at least 1.2 apart.
All inputs are finite; a program needn't handle non-finite values.
Results may differ from a plain program's by a relative error of at most 0.0003.
Values sent between devices are 32-bit elements; how exact they have to be, the bound alone decides.
A program may use at most 64 MiB of HBM per device.

v0:
```python
import math

import jax
import jax.numpy as jnp
from jax import lax
from jax.sharding import Mesh
from jax.sharding import PartitionSpec as P

ITERS = 3
ROOT_STEPS = 30
WIDE_NARROW = ("wide_0", "wide_1", "narrow_0", "narrow_1")
NARROW = ("narrow_0", "narrow_1")
WIDE = ("wide_0", "wide_1")


highest = lax.Precision.HIGHEST


def from_everyone(value, axis):
    devices = lax.axis_size(axis)
    return lax.all_to_all(
        jnp.broadcast_to(value[None], (devices, *value.shape)), axis, 0, 0, tiled=True
    )


def over_copies(value, axis):
    everything = from_everyone(value, axis)
    return jnp.sum(everything, axis=0)


def by_axis(value, axes):
    far, near = axes
    return over_copies(over_copies(value, near), far)


def in_order(blocks, dim):
    blocks = jnp.moveaxis(blocks, 0, dim)
    lengths = blocks.shape
    return blocks.reshape(*lengths[:dim], lengths[dim] * lengths[dim + 1], *lengths[dim + 2 :])


def gather_directly(value, axis, dim):
    return in_order(from_everyone(value, axis), dim)


def split_up(value, dim, devices):
    before, after = (value.shape[:dim], value.shape[dim + 1 :])
    return jnp.moveaxis(value.reshape(*before, devices, -1, *after), dim, 0)


def sent_and_summed(value, axis, dim):
    blocks = split_up(value, dim, lax.axis_size(axis))
    arrived = lax.all_to_all(blocks, axis, split_axis=0, concat_axis=0, tiled=True)
    return arrived.sum(axis=0)


def tile_factors(dist_sq, itself):
    safe_sq = jnp.where(itself, 4.0, dist_sq)
    radial = jnp.sqrt(safe_sq)
    inverse = 1.0 / radial
    far_scalar = 0.75 * inverse + 0.5 * inverse * inverse * inverse
    far_outer = (0.75 * inverse - 1.5 * inverse * inverse * inverse) * inverse * inverse
    near_scalar = 1.0 - 0.28125 * radial
    near_outer = 0.09375 * inverse
    nearby = radial < 2.0
    scalar = jnp.where(itself, 1.0, jnp.where(nearby, near_scalar, far_scalar))
    outer_part = jnp.where(itself, 0.0, jnp.where(nearby, near_outer, far_outer))
    return (scalar, outer_part)


def contract(left, kernel):
    return lax.dot_general(
        left,
        kernel,
        (((1,), (1,)), ((), ())),
        precision=highest,
        preferred_element_type=jnp.float32,
    )


def tile_product(row_pos, row_ids, col_pos, col_ids, vectors):
    width = vectors.shape[1]
    delta = row_pos[:, :, None] - col_pos[:, None, :]
    dist_sq = delta[0] * delta[0] + delta[1] * delta[1] + delta[2] * delta[2]
    itself = row_ids[:, None] == col_ids[None, :]
    scalar, outer_part = tile_factors(dist_sq, itself)
    result = []
    for component in range(3):
        diag_kernel = scalar + outer_part * delta[component] * delta[component]
        result.append(contract(vectors[component], diag_kernel))
    for first, second in ((0, 1), (0, 2), (1, 2)):
        cross = outer_part * delta[first] * delta[second]
        both = contract(jnp.concatenate([vectors[second], vectors[first]], axis=0), cross)
        result[first] = result[first] + both[:width]
        result[second] = result[second] + both[width:]
    return jnp.stack(result)


def blocked_product(row_pos, row_ids, col_pos, col_ids, vectors):
    rows = row_pos.shape[1]
    block = math.gcd(rows, 512)

    def row_block(index):
        begin = index * block
        pos_block = lax.dynamic_slice_in_dim(row_pos, begin, block, 1)
        id_block = lax.dynamic_slice_in_dim(row_ids, begin, block, 0)
        return tile_product(pos_block, id_block, col_pos, col_ids, vectors)

    pieces = lax.map(row_block, jnp.arange(rows // block, dtype=jnp.int32))
    return jnp.moveaxis(pieces, 0, 2).reshape(3, vectors.shape[1], rows)


def gram_of(left, right):
    return jnp.einsum("asp,atp->st", left, right, precision=highest)


def stacked_gram(stacked, right):
    return jnp.einsum("kasp,atp->kst", stacked, right, precision=highest)


def stacked_remove(stacked, weights):
    return jnp.einsum("kasp,kst->atp", stacked, weights, precision=highest)


def rotate(block, matrix):
    return jnp.einsum("atp,ts->asp", block, matrix, precision=highest)


def cholesky_pair(gram):
    order = gram.shape[0]
    places = jnp.arange(order, dtype=jnp.int32)
    lower = jnp.zeros((order, order), jnp.float32)
    for column in range(order):
        needed = gram[:, column] - jnp.dot(
            lower, lower[column, :], precision=highest, preferred_element_type=jnp.float32
        )
        pivot = jnp.sqrt(needed[column])
        entries = jnp.where(places >= column, needed / pivot, 0.0)
        marker = (places == column).astype(jnp.float32)
        lower = lower + entries[:, None] * marker[None, :]
    solved = jnp.zeros((order, order), jnp.float32)
    for row in range(order):
        marker = (places == row).astype(jnp.float32)
        fresh = (
            marker
            - jnp.dot(lower[row, :], solved, precision=highest, preferred_element_type=jnp.float32)
        ) / lower[row, row]
        solved = solved + marker[:, None] * fresh[None, :]
    return (lower.T, solved.T)


def tridiagonal(diagonal_blocks, lower_blocks):
    width = diagonal_blocks[0].shape[0]
    order = len(diagonal_blocks) * width
    matrix = jnp.zeros((order, order), jnp.float32)
    for index, block in enumerate(diagonal_blocks):
        offset = index * width
        matrix = matrix.at[offset : offset + width, offset : offset + width].set(block)
    for index, block in enumerate(lower_blocks):
        offset = index * width
        matrix = matrix.at[offset + width : offset + 2 * width, offset : offset + width].set(block)
        matrix = matrix.at[offset : offset + width, offset + width : offset + 2 * width].set(
            block.T
        )
    return matrix


def matrix_root(matrix):
    identity = jnp.eye(matrix.shape[0], dtype=jnp.float32)
    scale = jnp.sqrt(jnp.sum(matrix * matrix))

    def newton(turn, carry):
        current, other = carry
        factor = 1.5 * identity - 0.5 * jnp.dot(
            other, current, precision=highest, preferred_element_type=jnp.float32
        )
        return (
            jnp.dot(current, factor, precision=highest, preferred_element_type=jnp.float32),
            jnp.dot(factor, other, precision=highest, preferred_element_type=jnp.float32),
        )

    current, other = lax.fori_loop(0, ROOT_STEPS, newton, (matrix / scale, identity))
    return current * jnp.sqrt(scale)


def first_pass(basis, image):
    stacked = jnp.stack(basis)
    projections = by_axis(
        stacked_gram(stacked, image), (("wide_0", "wide_1", "narrow_0"), "narrow_1")
    )
    return (projections[-1], image - stacked_remove(stacked, projections))


def second_pass(basis, work):
    stacked = jnp.stack(basis)
    again, raw_gram = (
        by_axis(stacked_gram(stacked, work), (("wide_0", "wide_1", "narrow_0"), "narrow_1")),
        by_axis(gram_of(work, work), (("wide_0", "wide_1", "narrow_0"), "narrow_1")),
    )
    work = work - stacked_remove(stacked, again)
    gram = raw_gram - jnp.einsum("kst,ksu->tu", again, again, precision=highest)
    return (work, gram)


def per_device(positions, noise):
    width = noise.shape[1]
    local = noise.shape[2]
    narrow_count = lax.axis_size(NARROW)
    row_pos = gather_directly(positions, NARROW, 1)
    col_pos = gather_directly(positions, WIDE, 1)
    row_ids = lax.axis_index(WIDE) * (narrow_count * local) + jnp.arange(
        narrow_count * local, dtype=jnp.int32
    )
    places = jnp.arange(col_pos.shape[1], dtype=jnp.int32)
    col_ids = (
        places // local * (narrow_count * local) + lax.axis_index(NARROW) * local + places % local
    )
    noise_gram = by_axis(gram_of(noise, noise), (("wide_0", "wide_1", "narrow_0"), "narrow_1"))
    start_upper, start_inverse = cholesky_pair(noise_gram)
    basis = [rotate(noise, start_inverse)]
    diagonal_blocks = []
    lower_blocks = []
    for index in range(ITERS):
        empty = jnp.zeros((3, width, row_pos.shape[1]), jnp.float32)
        partial_rows = empty + blocked_product(
            row_pos, row_ids, col_pos, col_ids, gather_directly(basis[index], WIDE, 2)
        )
        product = sent_and_summed(partial_rows, NARROW, 2)
        if index + 1 == ITERS:
            current_block = by_axis(
                gram_of(basis[index], product), (("wide_0", "wide_1", "narrow_0"), "narrow_1")
            )
            diagonal_blocks.append(0.5 * (current_block + current_block.T))
        else:
            current_block, work = first_pass(basis, product)
            diagonal_blocks.append(0.5 * (current_block + current_block.T))
            work, gram = second_pass(basis, work)
            upper, inverse = cholesky_pair(gram)
            lower_blocks.append(upper)
            basis.append(rotate(work, inverse))
    root = matrix_root(tridiagonal(diagonal_blocks, lower_blocks))
    mixing = jnp.dot(
        root[:, :width], start_upper, precision=highest, preferred_element_type=jnp.float32
    ).reshape(ITERS, width, width)
    return jnp.einsum("katp,kts->asp", jnp.stack(basis), mixing, precision=highest)


def solution(mesh):
    finer = Mesh(mesh.devices.reshape(4, 4, 4, 2), ("wide_0", "wide_1", "narrow_0", "narrow_1"))
    return jax.shard_map(
        per_device,
        mesh=finer,
        in_specs=(P(None, WIDE_NARROW), P(None, None, WIDE_NARROW)),
        out_specs=P(None, None, WIDE_NARROW),
        check_vma=False,
    )
```

profile of v0, /device:TPU:1, one launch (start us, length us, event | category | flops | bytes accessed | tf_op | source)
XLA Modules:
  0.0 629.5 jit_solution(3667694234580183160)
XLA Ops:
  9.4 11.2 %all-to-all-start.1 = ((f32[64,1,256]{2,1,0:T(1,128)}), f32[64,1,256]{2,1,0:T(1,128)S(1)}, u32[]{:S(2)}, u32[]{:S(2)}) async-start(f32[64,1,256]{2,1,0:T(1,128)} %reshape.1051), calls=%async_computation.1 | async-start | bytes 131072 | tf_op jit(solution)/shard_map/all_to_all | solution.py:21
  20.9 8.2 %all-to-all-done.1 = f32[64,1,256]{2,1,0:T(1,128)S(1)} async-done(((f32[64,1,256]{2,1,0:T(1,128)}), f32[64,1,256]{2,1,0:T(1,128)S(1)}, u32[]{:S(2)}, u32[]{:S(2)}) %all-to-all-start.1) | async-done | bytes 65568 | tf_op jit(solution)/shard_map/all_to_all | solution.py:21
  74.6 6.6 %all-to-all-start.4 = ((f32[16,3,16,128]{3,2,1,0:T(8,128)}), f32[16,3,16,128]{3,2,1,0:T(8,128)S(1)}, u32[]{:S(2)}, u32[]{:S(2)}) async-start(f32[16,3,16,128]{3,2,1,0:T(8,128)} %broadcast_in_dim.168), calls=%async_computation.4 | async-start | bytes 786432 | tf_op jit(solution)/shard_map/all_to_all | solution.py:21
  81.3 8.0 %all-to-all-done.4 = f32[16,3,16,128]{3,2,1,0:T(8,128)S(1)} async-done(((f32[16,3,16,128]{3,2,1,0:T(8,128)}), f32[16,3,16,128]{3,2,1,0:T(8,128)S(1)}, u32[]{:S(2)}, u32[]{:S(2)}) %all-to-all-start.4) | async-done | bytes 393248 | tf_op jit(solution)/shard_map/all_to_all | solution.py:21
  89.9 6.7 %all-to-all-start.2 = ((f32[8,3,128]{2,1,0:T(4,128)}), f32[8,3,128]{2,1,0:T(4,128)S(1)}, u32[]{:S(2)}, u32[]{:S(2)}) async-start(f32[8,3,128]{2,1,0:T(4,128)} %broadcast_in_dim.166), calls=%async_computation.2 | async-start | bytes 32768 | tf_op jit(solution)/shard_map/all_to_all | solution.py:21
  101.2 72.3 %while.56 = (s32[]{:T(128)}, f32[2,3,16,512]{3,2,1,0:T(8,128)S(1)}, s32[2]{0:T(128)S(1)}, s32[1024]{0:T(1024)S(1)}, f32[3,1024]{1,0:T(4,128)S(1)}, /*index=5*/f3...) while((s32[]{:T(128)}, f32[2,3,16,512]{3,2,1,0:T(8,128)S(1)}, ...), condition=%wide.region_3.4_spmd.clone, body=%wide.region_2.3_spmd.clone.sunk | while | flops 1879177216 | bytes 127822048 | solution.py:109
  173.9 9.0 %all_to_all.125 = f32[8,3,16,128]{3,2,1,0:T(8,128)S(1)} all-to-all(f32[8,3,16,128]{3,2,1,0:T(8,128)S(1)} %copy.167), channel_id=1, replica_groups=mesh['wide_0'=4,'wide_1'=4,'narrow_0'=4,'narrow_1'=2] {'narrow_0','narro..., dimensions={0} | all-to-all | bytes 393216 | tf_op jit(solution)/shard_map/all_to_all | solution.py:53
  188.7 13.3 %all_to_all.126 = f32[64,1,256]{2,1,0:T(1,128)S(1)} all-to-all(f32[64,1,256]{2,1,0:T(1,128)S(1)} %reshape.1055), channel_id=1, replica_groups=mesh['wide_0'=4,'wide_1'=4,'narrow_0'=4,'narrow_1'=2] {'wide_0','wide_1'..., dimensions={0} | all-to-all | bytes 131072 | tf_op jit(solution)/shard_map/all_to_all | solution.py:21
  204.4 5.1 all_to_all.121
  221.1 6.8 %all-to-all-done.9 = f32[64,1,256]{2,1,0:T(1,128)S(1)} async-done(((f32[64,1,256]{2,1,0:T(1,128)}), f32[64,1,256]{2,1,0:T(1,128)S(1)}, u32[]{:S(2)}, u32[]{:S(2)}) %all-to-all-start.9) | async-done | bytes 65568 | tf_op jit(solution)/shard_map/all_to_all | solution.py:21
  234.1 7.3 %all-to-all-done.11 = f32[64,1,256]{2,1,0:T(1,128)S(1)} async-done(((f32[64,1,256]{2,1,0:T(1,128)}), f32[64,1,256]{2,1,0:T(1,128)S(1)}, u32[]{:S(2)}, u32[]{:S(2)}) %all-to-all-start.11) | async-done | bytes 65568 | tf_op jit(solution)/shard_map/all_to_all | solution.py:21
  287.1 8.0 %all-to-all-done.12 = f32[16,3,16,128]{3,2,1,0:T(8,128)S(1)} async-done(((f32[16,3,16,128]{3,2,1,0:T(8,128)}), f32[16,3,16,128]{3,2,1,0:T(8,128)S(1)}, u32[]{:S(2)}, u32[]{:S(2)}) %all-to-all-start.12) | async-done | bytes 393248 | tf_op jit(solution)/shard_map/all_to_all | solution.py:21
  295.6 72.3 %while.57 = (s32[]{:T(128)}, f32[2,3,16,512]{3,2,1,0:T(8,128)S(1)}, s32[2]{0:T(128)S(1)}, s32[1024]{0:T(1024)S(1)}, f32[3,1024]{1,0:T(4,128)S(1)}, /*index=5*/f3...) while((s32[]{:T(128)}, f32[2,3,16,512]{3,2,1,0:T(8,128)S(1)}, ...), condition=%wide.region_12.13_spmd.clone, body=%wide.region_11.12_spmd.clone.sunk | while | flops 1879177216 | bytes 127822048 | solution.py:109
  368.3 11.9 %all_to_all.127 = f32[8,3,16,128]{3,2,1,0:T(8,128)S(1)} all-to-all(f32[8,3,16,128]{3,2,1,0:T(8,128)S(1)} %copy.181), channel_id=1, replica_groups=mesh['wide_0'=4,'wide_1'=4,'narrow_0'=4,'narrow_1'=2] {'narrow_0','narro..., dimensions={0} | all-to-all | bytes 393216 | tf_op jit(solution)/shard_map/all_to_all | solution.py:53
  386.2 13.4 %all_to_all.128 = f32[64,1,512]{2,1,0:T(1,128)S(1)} all-to-all(f32[64,1,512]{2,1,0:T(1,128)S(1)} %reshape.1067), channel_id=1, replica_groups=mesh['wide_0'=4,'wide_1'=4,'narrow_0'=4,'narrow_1'=2] {'wide_0','wide_1'..., dimensions={0} | all-to-all | bytes 262144 | tf_op jit(solution)/shard_map/all_to_all | solution.py:21
  401.8 5.1 all_to_all.123
  419.7 6.5 %all-to-all-done.17 = f32[64,1,256]{2,1,0:T(1,128)S(1)} async-done(((f32[64,1,256]{2,1,0:T(1,128)}), f32[64,1,256]{2,1,0:T(1,128)S(1)}, u32[]{:S(2)}, u32[]{:S(2)}) %all-to-all-start.17) | async-done | bytes 65568 | tf_op jit(solution)/shard_map/all_to_all | solution.py:21
  434.5 5.3 all-to-all-done.19
  486.1 5.8 all-to-all-done.20
  492.7 72.2 %while.58 = (s32[]{:T(128)}, f32[2,3,16,512]{3,2,1,0:T(8,128)S(1)}, s32[2]{0:T(128)S(1)}, s32[1024]{0:T(1024)S(1)}, f32[3,1024]{1,0:T(4,128)S(1)}, /*index=5*/f3...) while((s32[]{:T(128)}, f32[2,3,16,512]{3,2,1,0:T(8,128)S(1)}, ...), condition=%wide.region_21.22_spmd.clone, body=%wide.region_20.21_spmd.clone.sunk | while | flops 1879177216 | bytes 127822048 | solution.py:109
  566.1 7.3 %all-to-all-start.21 = ((f32[8,3,16,128]{3,2,1,0:T(8,128)}), f32[8,3,16,128]{3,2,1,0:T(8,128)S(1)}, u32[]{:S(2)}, u32[]{:S(2)}) async-start(f32[8,3,16,128]{3,2,1,0:T(8,128)} %copy.199), calls=%async_computation.21 | async-start | bytes 393216 | tf_op jit(solution)/shard_map/all_to_all | solution.py:53
  585.5 5.0 all-to-all-start.23
  591.5 7.4 %all-to-all-done.23 = f32[64,1,256]{2,1,0:T(1,128)S(1)} async-done(((f32[64,1,256]{2,1,0:T(1,128)}), f32[64,1,256]{2,1,0:T(1,128)S(1)}, u32[]{:S(2)}, u32[]{:S(2)}) %all-to-all-start.23) | async-done | bytes 65568 | tf_op jit(solution)/shard_map/all_to_all | solution.py:21
  610.2 18.0 %while.59 = (s32[]{:T(128)}, f32[48,48]{0,1:T(8,128)S(1)}, f32[48,48]{1,0:T(8,128)S(1)}, s32[]{:T(128)}) while((s32[]{:T(128)}, f32[48,48]{0,1:T(8,128)S(1)}, f32[48,48]{1,0:T(8,128)S(1)}, s32[]{:T(128)}) %tuple.235), condition=%wide.region_28.29_spmd.clone, body=%wide.region_27.28_spmd.clone.sunk | while | flops 3990530 | bytes 119861 | solution.py:182
  (995 shorter events, 427.3 us)
Async XLA Ops:
  1.6 5.6 all-to-all-start
  9.4 19.7 %all-to-all-start.1 = ((f32[64,1,256]{2,1,0:T(1,128)}), f32[64,1,256]{2,1,0:T(1,128)S(1)}, u32[]{:S(2)}, u32[]{:S(2)}) async-start(f32[64,1,256]{2,1,0:T(1,128)} %reshape.1051), calls=%async_computation.1 | async-start | bytes 131072 | tf_op jit(solution)/shard_map/all_to_all | solution.py:21
  30.4 43.3 %all-to-all-start.3 = ((f32[16,3,128]{2,1,0:T(4,128)}), f32[16,3,128]{2,1,0:T(4,128)S(1)}, u32[]{:S(2)}, u32[]{:S(2)}) async-start(f32[16,3,128]{2,1,0:T(4,128)} %broadcast_in_dim.167), calls=%async_computation.3 | async-start | bytes 65536 | tf_op jit(solution)/shard_map/all_to_all | solution.py:21
  74.6 14.6 %all-to-all-start.4 = ((f32[16,3,16,128]{3,2,1,0:T(8,128)}), f32[16,3,16,128]{3,2,1,0:T(8,128)S(1)}, u32[]{:S(2)}, u32[]{:S(2)}) async-start(f32[16,3,16,128]{3,2,1,0:T(8,128)} %broadcast_in_dim.168), calls=%async_computation.4 | async-start | bytes 786432 | tf_op jit(solution)/shard_map/all_to_all | solution.py:21
  89.9 11.3 %all-to-all-start.2 = ((f32[8,3,128]{2,1,0:T(4,128)}), f32[8,3,128]{2,1,0:T(4,128)S(1)}, u32[]{:S(2)}, u32[]{:S(2)}) async-start(f32[8,3,128]{2,1,0:T(4,128)} %broadcast_in_dim.166), calls=%async_computation.2 | async-start | bytes 32768 | tf_op jit(solution)/shard_map/all_to_all | solution.py:21
  209.5 5.2 all-to-all-start.10
  214.8 13.1 %all-to-all-start.9 = ((f32[64,1,256]{2,1,0:T(1,128)}), f32[64,1,256]{2,1,0:T(1,128)S(1)}, u32[]{:S(2)}, u32[]{:S(2)}) async-start(f32[64,1,256]{2,1,0:T(1,128)} %reshape.1063), calls=%async_computation.9 | async-start | bytes 131072 | tf_op jit(solution)/shard_map/all_to_all | solution.py:21
  227.9 13.4 %all-to-all-start.11 = ((f32[64,1,256]{2,1,0:T(1,128)}), f32[64,1,256]{2,1,0:T(1,128)S(1)}, u32[]{:S(2)}, u32[]{:S(2)}) async-start(f32[64,1,256]{2,1,0:T(1,128)} %reshape.1059), calls=%async_computation.11 | async-start | bytes 131072 | tf_op jit(solution)/shard_map/all_to_all | solution.py:21
  283.6 11.5 %all-to-all-start.12 = ((f32[16,3,16,128]{3,2,1,0:T(8,128)}), f32[16,3,16,128]{3,2,1,0:T(8,128)S(1)}, u32[]{:S(2)}, u32[]{:S(2)}) async-start(f32[16,3,16,128]{3,2,1,0:T(8,128)} %broadcast_in_dim.175), calls=%async_computation.12 | async-start | bytes 786432 | tf_op jit(solution)/shard_map/all_to_all | solution.py:21
  408.4 4.6 all-to-all-start.18
  413.0 13.2 %all-to-all-start.17 = ((f32[64,1,256]{2,1,0:T(1,128)}), f32[64,1,256]{2,1,0:T(1,128)S(1)}, u32[]{:S(2)}, u32[]{:S(2)}) async-start(f32[64,1,256]{2,1,0:T(1,128)} %reshape.1075), calls=%async_computation.17 | async-start | bytes 131072 | tf_op jit(solution)/shard_map/all_to_all | solution.py:21
  426.2 13.6 %all-to-all-start.19 = ((f32[64,1,512]{2,1,0:T(1,128)}), f32[64,1,512]{2,1,0:T(1,128)S(1)}, u32[]{:S(2)}, u32[]{:S(2)}) async-start(f32[64,1,512]{2,1,0:T(1,128)} %reshape.1071), calls=%async_computation.19 | async-start | bytes 262144 | tf_op jit(solution)/shard_map/all_to_all | solution.py:21
  480.3 11.5 %all-to-all-start.20 = ((f32[16,3,16,128]{3,2,1,0:T(8,128)}), f32[16,3,16,128]{3,2,1,0:T(8,128)S(1)}, u32[]{:S(2)}, u32[]{:S(2)}) async-start(f32[16,3,16,128]{3,2,1,0:T(8,128)} %broadcast_in_dim.182), calls=%async_computation.20 | async-start | bytes 786432 | tf_op jit(solution)/shard_map/all_to_all | solution.py:21
  492.5 98.0 %copy-start.9 = (f32[16]{0:T(128)S(1)}, f32[16]{0:T(128)}, u32[]{:S(2)}) copy-start(f32[16]{0:T(128)} %copy-done.6) | copy-start | bytes 196
  492.5 98.0 %copy-start.13 = (f32[16]{0:T(128)S(1)}, f32[16]{0:T(128)}, u32[]{:S(2)}) copy-start(f32[16]{0:T(128)} %copy-done.10) | copy-start | bytes 196
  492.5 98.0 %copy-start.17 = (f32[16]{0:T(128)S(1)}, f32[16]{0:T(128)}, u32[]{:S(2)}) copy-start(f32[16]{0:T(128)} %copy-done.14) | copy-start | bytes 196
  492.5 98.0 %copy-start.21 = (f32[16]{0:T(128)S(1)}, f32[16]{0:T(128)}, u32[]{:S(2)}) copy-start(f32[16]{0:T(128)} %copy-done.18) | copy-start | bytes 196
  492.5 98.0 %copy-start.25 = (f32[16]{0:T(128)S(1)}, f32[16]{0:T(128)}, u32[]{:S(2)}) copy-start(f32[16]{0:T(128)} %copy-done.22) | copy-start | bytes 196
  492.5 98.0 %copy-start.29 = (f32[16]{0:T(128)S(1)}, f32[16]{0:T(128)}, u32[]{:S(2)}) copy-start(f32[16]{0:T(128)} %copy-done.26) | copy-start | bytes 196
  492.5 98.0 %copy-start.37 = (f32[16]{0:T(128)S(1)}, f32[16]{0:T(128)}, u32[]{:S(2)}) copy-start(f32[16]{0:T(128)} %copy-done.34) | copy-start | bytes 196
  492.5 98.0 %copy-start.41 = (f32[16]{0:T(128)S(1)}, f32[16]{0:T(128)}, u32[]{:S(2)}) copy-start(f32[16]{0:T(128)} %copy-done.38) | copy-start | bytes 196
  492.5 98.0 %copy-start.45 = (f32[16]{0:T(128)S(1)}, f32[16]{0:T(128)}, u32[]{:S(2)}) copy-start(f32[16]{0:T(128)} %copy-done.42) | copy-start | bytes 196
  566.1 13.2 %all-to-all-start.21 = ((f32[8,3,16,128]{3,2,1,0:T(8,128)}), f32[8,3,16,128]{3,2,1,0:T(8,128)S(1)}, u32[]{:S(2)}, u32[]{:S(2)}) async-start(f32[8,3,16,128]{3,2,1,0:T(8,128)} %copy.199), calls=%async_computation.21 | async-start | bytes 393216 | tf_op jit(solution)/shard_map/all_to_all | solution.py:53
  585.5 13.4 %all-to-all-start.23 = ((f32[64,1,256]{2,1,0:T(1,128)}), f32[64,1,256]{2,1,0:T(1,128)S(1)}, u32[]{:S(2)}, u32[]{:S(2)}) async-start(f32[64,1,256]{2,1,0:T(1,128)} %reshape.1079), calls=%async_computation.23 | async-start | bytes 131072 | tf_op jit(solution)/shard_map/all_to_all | solution.py:21
  (142 other events, 7292.3 us)
where the time goes:
time: 637 us; the launch traced here: 630 us
  matrix products  215 us (34%)
  other arithmetic  83.5 us (13%)
  starting transfers between devices  78.4 us (12%)
  waiting for transfers between devices  72.9 us (11%)
  blocking collectives  70.8 us (11%)
  local copies, waits for them, and re-layouts  64.8 us (10%)
  between operations  36.4 us (6%)
  loops' own time  8.08 us (1%)
    dot_general x36, matrix products, contract(): lax.dot_general(left, kernel, (((1,), (1,)), ((), ())), precision=highest...  148 us
    all_to_all x14, starting transfers between devices, from_everyone(): lax.all_to_all(jnp.broadcast_to(value[None], (devices, *value.shape)), ax...  71.1 us
    all_to_all x14, waiting for transfers between devices, from_everyone(): lax.all_to_all(jnp.broadcast_to(value[None], (devices, *value.shape)), ax...  68.5 us
    select_n x12, other arithmetic, tile_factors(): jnp.where(itself, 0.0, jnp.where(nearby, near_outer, far_outer))  52.3 us
    all_to_all x7, blocking collectives, from_everyone(): lax.all_to_all(jnp.broadcast_to(value[None], (devices, *value.shape)), ax...  49.9 us
    dot_general x48, matrix products, cholesky_pair(): jnp.dot(lower[row, :], solved, precision=highest, preferred_element_type=...  39.3 us
    slice x45, local copies, waits for them, and re-layouts, cholesky_pair(): pivot = jnp.sqrt(needed[column])  28.4 us
    all_to_all x2, blocking collectives, sent_and_summed(): lax.all_to_all(blocks, axis, split_axis=0, concat_axis=0, tiled=True)  20.9 us
  transfers between devices with their start and end apart: 15, of which 13 were waited for; matrix products, arithmetic and copies ran while one was open for 7% of the time, Pallas kernels for 0%

commit v1 on v0

v1 whole, which is shorter than its diff:
```python
import functools

import jax
import jax.numpy as jnp
from jax import lax
from jax.experimental import pallas as pl
from jax.experimental.pallas import tpu as pltpu
from jax.sharding import PartitionSpec as P

ROOT_STEPS = 30
NW = 16
NN = 8
S = 16
L = 128
CENTRE = 34.0
MESH = pl.DeviceIdType.MESH
HI = lax.Precision.HIGHEST
F32 = jnp.float32
BF16 = jnp.bfloat16


def mm(a, b):
    return lax.dot_general(a, b, (((1,), (0,)), ((), ())), precision=HI, preferred_element_type=F32)


def mt(a, b):
    return lax.dot_general(a, b, (((1,), (1,)), ((), ())), precision=HI, preferred_element_type=F32)


def eye(n):
    return (lax.broadcasted_iota(jnp.int32, (n, n), 0) == lax.broadcasted_iota(jnp.int32, (n, n), 1)).astype(F32)


def transposed(a):
    return mt(eye(a.shape[1]), a)


def cholesky_pair(gram):
    n = gram.shape[0]
    rows = lax.broadcasted_iota(jnp.int32, (n, n), 0)
    cols = lax.broadcasted_iota(jnp.int32, (n, n), 1)
    left, right = gram, eye(n)
    upper, inverse = jnp.zeros((n, n), F32), jnp.zeros((n, n), F32)
    for c in range(n):
        scale = lax.rsqrt(jnp.broadcast_to(left[c : c + 1, c : c + 1], (1, n)))
        row = left[c : c + 1, :] * scale
        other = right[c : c + 1, :] * scale
        upper = jnp.where((rows == c) & (cols >= c), jnp.broadcast_to(row, (n, n)), upper)
        inverse = jnp.where((rows == c) & (cols <= c), jnp.broadcast_to(other, (n, n)), inverse)
        if c + 1 < n:
            factor = jnp.broadcast_to(left[:, c : c + 1], (n, n)) * scale
            left = left - factor * row
            right = right - jnp.where(rows > c, factor * other, 0.0)
    return upper, inverse


def split(value):
    high = value.astype(BF16)
    low = (value - high.astype(F32)).astype(BF16)
    return high, low


def main_kernel(
    pos_ref,
    noise_ref,
    vec_ref,
    small_ref,
    tot_ref,
    ztot_ref,
    cpos,
    rpos,
    xg0,
    xg1,
    xg2,
    xr,
    pb1,
    pb2,
    rb1,
    rb2,
    pz,
    lhi,
    llo,
    rmat,
    acc,
    accl,
    xjb,
    ga1,
    gb1,
    ga2,
    gb2,
    za,
    zb,
    send_w,
    recv_w,
    send_n,
    recv_n,
):
    w = lax.axis_index("wide")
    n = lax.axis_index("narrow")

    def wide_copy(phase, src, dst, target, slot):
        return pltpu.make_async_remote_copy(
            src_ref=src,
            dst_ref=dst.at[slot],
            send_sem=send_w.at[phase, target],
            recv_sem=recv_w.at[phase, slot],
            device_id={"wide": target},
            device_id_type=MESH,
        )

    def narrow_copy(phase, src, dst, target, slot):
        return pltpu.make_async_remote_copy(
            src_ref=src,
            dst_ref=dst.at[slot],
            send_sem=send_n.at[phase, target],
            recv_sem=recv_n.at[phase, slot],
            device_id={"narrow": target},
            device_id_type=MESH,
        )

    def loop(count, body):
        def step(i, carry):
            body(i)
            return carry

        lax.fori_loop(0, count, step, 0)

    def wide_send(phase, dst):
        loop(NW - 1, lambda p: wide_copy(phase, dst.at[w], dst, lax.rem(w + p + 1, NW), w).start())

    def wide_recv(phase, dst):
        def one(p):
            s = lax.rem(w + p + 1, NW)
            wide_copy(phase, dst.at[s], dst, s, s).wait_recv()

        loop(NW - 1, one)

    def wide_sent(phase, dst):
        def one(p):
            s = lax.rem(w + p + 1, NW)
            wide_copy(phase, dst.at[w], dst, s, w).wait_send()

        loop(NW - 1, one)

    def narrow_send(phase, dst, scatter=None):
        def one(p):
            t = lax.rem(n + p + 1, NN)
            narrow_copy(phase, dst.at[n] if scatter is None else scatter.at[t], dst, t, n).start()

        loop(NN - 1, one)

    def narrow_recv(phase, dst):
        def one(p):
            s = lax.rem(n + p + 1, NN)
            narrow_copy(phase, dst.at[s], dst, s, s).wait_recv()

        loop(NN - 1, one)

    def narrow_sent(phase, dst):
        def one(p):
            s = lax.rem(n + p + 1, NN)
            narrow_copy(phase, dst.at[n], dst, s, n).wait_send()

        loop(NN - 1, one)

    def all_of(buffer, count):
        total = buffer[0]
        for i in range(1, count):
            total = total + buffer[i]
        return total

    barrier = pltpu.get_barrier_semaphore()

    def greet_wide(p):
        pl.semaphore_signal(barrier, inc=1, device_id={"wide": lax.rem(w + p + 1, NW)}, device_id_type=MESH)

    def greet_narrow(p):
        pl.semaphore_signal(barrier, inc=1, device_id={"narrow": lax.rem(n + p + 1, NN)}, device_id_type=MESH)

    loop(NW - 1, greet_wide)
    loop(NN - 1, greet_narrow)
    own_pos = jnp.concatenate([pos_ref[...], jnp.zeros((5, L), F32)], axis=0)
    cpos[w] = own_pos
    rpos[n] = own_pos
    xg0[w] = noise_ref[...]
    za[n] = jnp.zeros((S, L), F32)
    pl.semaphore_wait(barrier, NW + NN - 2)

    wide_send(0, cpos)
    narrow_send(0, rpos)
    wide_send(1, xg0)
    narrow_recv(0, rpos)
    wide_recv(0, cpos)

    def build(jb):
        columns = cpos[jb].T
        for c in range(3):
            xjb[c] = jnp.broadcast_to(columns[:, c : c + 1], (L, L))

        def rows_of(ic):
            for half in range(2):
                ib = ic * 2 + half
                xi = [jnp.broadcast_to(rpos[ib, c : c + 1, :], (16, L)) for c in range(3)]
                lanes = pl.ds(pl.multiple_of(ib * L, L), L)
                for jt in range(8):
                    d = [xi[c] - xjb[c, jt * 16 : jt * 16 + 16, :] for c in range(3)]
                    sq = jnp.maximum(d[0] * d[0] + d[1] * d[1] + d[2] * d[2], 1e-20)
                    inv = lax.rsqrt(sq)
                    inv2 = inv * inv
                    near = sq < 4.0
                    iso = jnp.where(near, 1.0 - 0.28125 * (sq * inv), inv * (0.75 + 0.5 * inv2))
                    outer = inv * jnp.where(near, 0.09375, inv2 * (0.75 - 1.5 * inv2))
                    places = pl.ds(pl.multiple_of(jb * L + jt * 16, 16), 16)
                    for k, value in enumerate([outer * d[0], outer * d[1], outer * d[2], iso]):
                        high, low = split(value)
                        lhi[k, places, lanes] = high
                        llo[k, places, lanes] = low

        loop(NN // 2, rows_of)

    loop(NW, build)

    def product(xg, out):
        def expand(jb):
            lanes = pl.ds(pl.multiple_of(jb * L, L), L)
            x = [cpos[jb, c : c + 1, :] - CENTRE for c in range(3)]
            v = [xg[jb, e] for e in range(3)]
            pieces = [jnp.concatenate([v[e], x[0] * v[e], x[1] * v[e], x[2] * v[e]], axis=0) for e in range(3)]
            pieces.append(jnp.concatenate([jnp.zeros((S, L), F32), -v[0], -v[1], -v[2]], axis=0))
            for k in range(4):
                high, low = split(pieces[k])
                rmat[k, 0:64, lanes] = high
                rmat[k, 64:128, lanes] = low

        loop(NW, expand)
        acc[...] = jnp.zeros_like(acc)
        accl[...] = jnp.zeros_like(accl)

        def multiply(k):
            acc[...] += jnp.dot(rmat[k], lhi[k], preferred_element_type=F32)
            accl[...] += jnp.dot(rmat[k, 0:64, :], llo[k], preferred_element_type=F32)

        loop(4, multiply)
        for b in range(NN):
            lanes = slice(b * L, b * L + L)
            total = acc[0:64, lanes] + (acc[64:128, lanes] + accl[:, lanes])
            for c in range(3):
                out[b, c] = (rpos[b, c : c + 1, :] - CENTRE) * total[0:16] - total[16 + 16 * c : 32 + 16 * c]

    lane = lax.broadcasted_iota(jnp.int32, (S, L), 1)

    wide_recv(1, xg0)
    product(xg0, pb1)
    rb1[n] = pb1[n]
    narrow_send(1, rb1, pb1)
    narrow_recv(1, rb1)
    xg1[w] = all_of(rb1, NN)
    wide_send(2, xg1)

    part = jnp.zeros((2 * S, L), F32)
    for c in range(3):
        a, b = noise_ref[c], xg1[w, c]
        part = part + mt(jnp.concatenate([a, b], axis=0), jnp.concatenate([a, b, b, b, b, b, b, b], axis=0))
    ga1[n] = jnp.where(lane < 32, part[0:16], part[16:32])
    narrow_send(2, ga1)
    narrow_recv(2, ga1)
    gb1[w] = all_of(ga1, NN)
    wide_send(3, gb1)

    wide_recv(2, xg1)
    product(xg1, pb2)
    rb2[n] = pb2[n]
    narrow_send(3, rb2, pb2)
    narrow_recv(3, rb2)
    y1 = all_of(rb2, NN)
    xg2[w] = y1
    xr[n] = y1
    wide_send(4, xg2)
    narrow_send(4, xr)

    wide_recv(3, gb1)
    total = all_of(gb1, NW)
    g00, g01, g11 = total[:, 0:16], total[:, 16:32], total[:, 32:48]
    upper0, inv0 = cholesky_pair(g00)

    def inside(g):
        return mt(mm(inv0, g), inv0)

    h1, c11, k1 = inside(g01), inside(g00), inside(g11)
    f1 = h1 + (h1 - mm(c11, h1))
    f1t = transposed(f1)
    fh = mm(f1t, h1)
    gram = k1 - fh - transposed(fh) + mm(f1t, mm(c11, f1))
    upper1, inv1 = cholesky_pair(gram)
    p21t = mm(inv1, inv0)
    p20t = -mm(mm(inv1, f1t), inv0)
    for c in range(3):
        a, b, d = noise_ref[c], xg1[w, c], xg2[w, c]
        vec_ref[0, c] = mm(inv0, a)
        vec_ref[1, c] = mm(p20t, a) + mm(p21t, b)
        vec_ref[2, c] = mm(p20t, b) + mm(p21t, d)
    for i, value in enumerate([upper0, upper1, h1, f1, p20t, p21t]):
        small_ref[i] = value

    part = jnp.zeros((5 * S, L), F32)
    for c in range(3):
        q1, q2, wv, y0, y1 = vec_ref[0, c], vec_ref[1, c], vec_ref[2, c], xg1[w, c], xg2[w, c]
        part = part + mt(
            jnp.concatenate([q1, q2, wv, y0, y1], axis=0), jnp.concatenate([q1, q2, wv, q2, wv, wv, y1, y1], axis=0)
        )
    packed = jnp.where(lane < 48, part[0:16], part[16:32])
    packed = jnp.where(lane < 80, packed, part[32:48])
    packed = jnp.where(lane < 96, packed, part[48:64])
    ga2[n] = jnp.where(lane < 112, packed, part[64:80])
    narrow_send(5, ga2)
    narrow_recv(5, ga2)
    gb2[w] = all_of(ga2, NN)
    wide_send(5, gb2)

    wide_recv(4, xg2)
    product(xg2, pz)
    narrow_recv(4, xr)
    part = jnp.zeros((S, S), F32)
    for c in range(3):
        part = part + mt(
            jnp.concatenate([xr[b, c] for b in range(NN)], axis=1), jnp.concatenate([pz[b, c] for b in range(NN)], axis=1)
        )
    za[n, :, 0:16] = part
    narrow_send(6, za)
    narrow_recv(6, za)
    zb[w] = all_of(za, NN)
    wide_send(6, zb)
    wide_recv(5, gb2)
    tot_ref[...] = all_of(gb2, NW)
    wide_recv(6, zb)
    ztot_ref[...] = all_of(zb, NW)

    for phase, buffer in enumerate([cpos, xg0, xg1, gb1, xg2, gb2, zb]):
        wide_sent(phase, buffer)
    for phase, buffer in enumerate([rpos, rb1, ga1, rb2, xr, ga2, za]):
        narrow_sent(phase, buffer)


def last_kernel(vec_ref, small_ref, tot_ref, ztot_ref, out_ref, y_ref, z_ref):
    upper0, upper1, h1, f1, p20t, p21t = [small_ref[i] for i in range(6)]
    total = tot_ref[...]
    c11, c12, ha, c22, hb, k, g12, g22 = [total[:, 16 * i : 16 * i + 16] for i in range(8)]
    zraw = ztot_ref[:, 0:16]
    p20, p21 = transposed(p20t), transposed(p21t)
    ga = ha - mm(c11, ha) - mm(c12, hb)
    gb = hb - mm(transposed(c12), ha) - mm(c22, hb)
    fa, fb = ha + ga, hb + gb
    fat, fbt = transposed(fa), transposed(fb)
    hat, hbt = transposed(ha), transposed(hb)
    fh = mm(fat, ha) + mm(fbt, hb)
    cf = mm(fat, mm(c11, fa) + mm(c12, fb)) + mm(fbt, mm(transposed(c12), fa) + mm(c22, fb))
    upper2, inv2 = cholesky_pair(k - fh - transposed(fh) + cf)
    zz = mm(p20t, mm(g12, p20) + mm(g22, p21)) + mm(p21t, mm(g22, p20) + mm(zraw, p21))
    wmq1 = mm(hat, f1) + mm(hbt, upper1)
    side = mm(wmq1, fa) + mm(k, fb)
    inner = zz - side - transposed(side) + mm(fat, mm(h1, fa) + mm(ha, fb)) + mm(fbt, mm(hat, fa) + mm(hb, fb))
    a3 = mt(mm(inv2, inner), inv2)

    def sym(a):
        return 0.5 * (a + transposed(a))

    order = 3 * S
    tri = jnp.zeros((order, order), F32)
    low = [
        (lax.broadcasted_iota(jnp.int32, (order, S), 0) == lax.broadcasted_iota(jnp.int32, (order, S), 1) + S * i).astype(F32)
        for i in range(3)
    ]
    blocks = [(0, 0, sym(h1)), (1, 1, sym(hb)), (2, 2, sym(a3)), (1, 0, upper1), (2, 1, upper2)]
    blocks += [(0, 1, transposed(upper1)), (1, 2, transposed(upper2))]
    for i, j, block in blocks:
        tri = tri + mt(mm(low[i], block), low[j])
    scale = jnp.sqrt(jnp.sum(tri * tri))
    ident = eye(order)
    y_ref[...] = tri / scale
    z_ref[...] = ident

    def more(carry):
        step, gap = carry
        return jnp.logical_and(step < ROOT_STEPS, jnp.logical_not(gap < 1e-8))

    def newton(carry):
        step, _ = carry
        y, z = y_ref[...], z_ref[...]
        zy = mm(z, y)
        factor = 1.5 * ident - 0.5 * zy
        y_ref[...] = mm(y, factor)
        z_ref[...] = mm(factor, z)
        off = zy - ident
        return step + 1, jnp.sum(off * off)

    lax.while_loop(more, newton, (jnp.int32(0), jnp.float32(1.0)))
    root = y_ref[...] * jnp.sqrt(scale)
    mixing = mm(transposed(upper0), mt(transposed(low[0]), root))
    for c in range(3):
        q1, q2, wv = vec_ref[0, c], vec_ref[1, c], vec_ref[2, c]
        q3 = mm(inv2, wv - mm(fat, q1) - mm(fbt, q2))
        out_ref[c] = mm(mixing, jnp.concatenate([q1, q2, q3], axis=0))


def per_device(positions, noise):
    block = (3, S, L)
    vmem = pl.BlockSpec(memory_space=pltpu.VMEM)
    vec, small, tot, ztot = pl.pallas_call(
        main_kernel,
        out_shape=[
            jax.ShapeDtypeStruct((3, *block), F32),
            jax.ShapeDtypeStruct((6, S, S), F32),
            jax.ShapeDtypeStruct((S, L), F32),
            jax.ShapeDtypeStruct((S, L), F32),
        ],
        in_specs=[vmem] * 2,
        out_specs=[vmem] * 4,
        scratch_shapes=[
            pltpu.VMEM((NW, 8, L), F32),
            pltpu.VMEM((NN, 8, L), F32),
            pltpu.VMEM((NW, *block), F32),
            pltpu.VMEM((NW, *block), F32),
            pltpu.VMEM((NW, *block), F32),
            pltpu.VMEM((NN, *block), F32),
            pltpu.VMEM((NN, *block), F32),
            pltpu.VMEM((NN, *block), F32),
            pltpu.VMEM((NN, *block), F32),
            pltpu.VMEM((NN, *block), F32),
            pltpu.VMEM((NN, *block), F32),
            pltpu.VMEM((4, NW * L, NN * L), BF16),
            pltpu.VMEM((4, NW * L, NN * L), BF16),
            pltpu.VMEM((4, L, NW * L), BF16),
            pltpu.VMEM((L, NN * L), F32),
            pltpu.VMEM((64, NN * L), F32),
            pltpu.VMEM((3, L, L), F32),
            pltpu.VMEM((NN, S, L), F32),
            pltpu.VMEM((NW, S, L), F32),
            pltpu.VMEM((NN, S, L), F32),
            pltpu.VMEM((NW, S, L), F32),
            pltpu.VMEM((NN, S, L), F32),
            pltpu.VMEM((NW, S, L), F32),
            pltpu.SemaphoreType.DMA((7, NW)),
            pltpu.SemaphoreType.DMA((7, NW)),
            pltpu.SemaphoreType.DMA((7, NN)),
            pltpu.SemaphoreType.DMA((7, NN)),
        ],
        compiler_params=pltpu.CompilerParams(
            collective_id=0, has_side_effects=True, vmem_limit_bytes=56 * 1024 * 1024
        ),
        name="lanczos",
    )(positions, noise)
    return pl.pallas_call(
        last_kernel,
        out_shape=jax.ShapeDtypeStruct(block, F32),
        in_specs=[vmem] * 4,
        out_specs=vmem,
        scratch_shapes=[pltpu.VMEM((3 * S, 3 * S), F32), pltpu.VMEM((3 * S, 3 * S), F32)],
        name="finish",
    )(vec, small, tot, ztot)


def solution(mesh):
    axes = ("wide", "narrow")
    return jax.shard_map(
        per_device,
        mesh=mesh,
        in_specs=(P(None, axes), P(None, None, axes)),
        out_specs=P(None, None, axes),
        check_vma=False,
    )
```

time: 637 us -> 106 us (0.17); the launches traced: 630 us -> 106 us
  matrix products: 215 us -> 0 us
  Pallas kernels: 0 us -> 106 us
  other arithmetic: 83.5 us -> 0 us
  starting transfers between devices: 78.4 us -> 0 us
  waiting for transfers between devices: 72.9 us -> 0 us
  blocking collectives: 70.8 us -> 0 us
  local copies, waits for them, and re-layouts: 64.8 us -> 0 us
  between operations: 36.4 us -> 0.01 us
  loops' own time: 8.08 us -> 0 us
    dot_general x239 -> x0, matrix products: 215 us -> none  [the longest x36 148 us: contract(): lax.dot_general(left, kernel, (((1,), (1,)), ((), ())), precision=highest...]
    pallas_call x0 -> x2, Pallas kernels: none -> 106 us  [the longest x1 94.7 us: per_device(): pl.pallas_call(main_kernel, out_shape=[jax.ShapeDtypeStruct((3, *block),...]
    all_to_all x15 -> x0, starting transfers between devices: 78.4 us -> none  [the longest x14 71.1 us: from_everyone(): lax.all_to_all(jnp.broadcast_to(value[None], (devices, *value.shape)), ax...]
    all_to_all x15 -> x0, waiting for transfers between devices: 72.9 us -> none  [the longest x14 68.5 us: from_everyone(): lax.all_to_all(jnp.broadcast_to(value[None], (devices, *value.shape)), ax...]
    all_to_all x9 -> x0, blocking collectives: 70.8 us -> none  [the longest x7 49.9 us: from_everyone(): lax.all_to_all(jnp.broadcast_to(value[None], (devices, *value.shape)), ax...]
    select_n x57 -> x0, other arithmetic: 52.5 us -> none  [the longest x12 52.3 us: tile_factors(): jnp.where(itself, 0.0, jnp.where(nearby, near_outer, far_outer))]
    slice x62 -> x0, local copies, waits for them, and re-layouts: 31.5 us -> none  [the longest x45 28.4 us: cholesky_pair(): pivot = jnp.sqrt(needed[column])]
    unnamed x346 -> x0, local copies, waits for them, and re-layouts: 13.4 us -> none
  transfers between devices with their start and end apart: 15 -> 0, of which waited for: 13 -> 0; matrix products, arithmetic and copies ran while one was open for 7% -> 0% of each run, Pallas kernels for 0% -> 0%
where the time goes in v1:
time: 106 us
  Pallas kernels  106 us (100%)
    pallas_call x1, Pallas kernels, per_device(): pl.pallas_call(main_kernel, out_shape=[jax.ShapeDtypeStruct((3, *block),...  94.7 us
    pallas_call x1, Pallas kernels, per_device(): pl.pallas_call(last_kernel, out_shape=jax.ShapeDtypeStruct(block, F32), i...  11.5 us

profile of v1, /device:TPU:1, one launch (start us, length us, event | category | flops | bytes accessed | tf_op | source)
XLA Modules:
  0.0 106.2 jit_solution(16450314136953346104)
XLA Ops:
  0.0 94.7 %lanczos.1 = (f32[3,3,16,128]{3,2,1,0:T(8,128)}, f32[6,16,16]{2,1,0:T(8,128)}, f32[16,128]{1,0:T(8,128)}, f32[16,128]{1,0:T(8,128)}) custom-call(f32[3,128]{1,0:T(4,128)} %pos_ref.1, f32[3,16,128]{2,1,0:T(8,128)} %noise_ref.1), custom_call_target="tpu_custom_call" | custom-call | tf_op jit(solution)/shard_map/lanczos/pallas_call | solution.py:408
  94.7 11.5 %finish.1 = f32[3,16,128]{2,1,0:T(8,128)} custom-call(f32[3,3,16,128]{3,2,1,0:T(8,128)} %get-tuple-element.9.vec_ref, f32[6,16,16]{2,1,0:T(8,128)} %get-tuple-element.10.small_ref, f32[16,128]{1,0:T(8,128)} %get-tuple-element.11.tot_ref, f32[16,128]{1,0:T(8,128)} %get-tuple-element.12.ztot_ref), custom_call_target="tpu_custom_call" | custom-call | tf_op jit(solution)/shard_map/finish/pallas_call | solution.py:452

commit v2 on v1

v2 whole, which is shorter than its diff:
```python
import functools

import jax
import jax.numpy as jnp
from jax import lax
from jax.experimental import pallas as pl
from jax.experimental.pallas import tpu as pltpu
from jax.sharding import PartitionSpec as P

ROOT_STEPS = 30
NW = 16
NN = 8
S = 16
L = 128
CENTRE = 34.0
MESH = pl.DeviceIdType.MESH
HI = lax.Precision.HIGHEST
F32 = jnp.float32
BF16 = jnp.bfloat16


def mm(a, b):
    return lax.dot_general(a, b, (((1,), (0,)), ((), ())), precision=HI, preferred_element_type=F32)


def mt(a, b):
    return lax.dot_general(a, b, (((1,), (1,)), ((), ())), precision=HI, preferred_element_type=F32)


def eye(n):
    return (lax.broadcasted_iota(jnp.int32, (n, n), 0) == lax.broadcasted_iota(jnp.int32, (n, n), 1)).astype(F32)


def transposed(a):
    return mt(eye(a.shape[1]), a)


def cholesky_pair(gram):
    n = gram.shape[0]
    rows = lax.broadcasted_iota(jnp.int32, (n, n), 0)
    cols = lax.broadcasted_iota(jnp.int32, (n, n), 1)
    left, right = gram, eye(n)
    upper, inverse = jnp.zeros((n, n), F32), jnp.zeros((n, n), F32)
    for c in range(n):
        scale = lax.rsqrt(jnp.broadcast_to(left[c : c + 1, c : c + 1], (1, n)))
        row = left[c : c + 1, :] * scale
        other = right[c : c + 1, :] * scale
        upper = jnp.where((rows == c) & (cols >= c), jnp.broadcast_to(row, (n, n)), upper)
        inverse = jnp.where((rows == c) & (cols <= c), jnp.broadcast_to(other, (n, n)), inverse)
        if c + 1 < n:
            factor = jnp.broadcast_to(left[:, c : c + 1], (n, n)) * scale
            left = left - factor * row
            right = right - jnp.where(rows > c, factor * other, 0.0)
    return upper, inverse


def split(value):
    high = value.astype(BF16)
    low = (value - high.astype(F32)).astype(BF16)
    return high, low


def hops(offset):
    return sum(min(part, 4 - part) for part in offset)


OFFSETS = sorted([(a, b) for a in range(4) for b in range(4)], key=hops)


def main_kernel(
    pos_hbm,
    noise_hbm,
    vec_ref,
    tri_ref,
    mix_ref,
    low_ref,
    ztot_ref,
    cpos,
    rpos,
    xg0,
    xg1,
    xg2,
    xr,
    pb1,
    pb2,
    rb1,
    rb2,
    pz,
    lhi,
    llo,
    rmat,
    acc,
    accl,
    xjb,
    ga1,
    gb1,
    ga2,
    gb2,
    za,
    zb,
    send_b,
    recv_b,
    send_w,
    recv_w,
    send_n,
    recv_n,
    load_sem,
):
    w = lax.axis_index("wide")
    n = lax.axis_index("narrow")

    def loop(begin, end, body):
        def step(i, carry):
            body(i)
            return carry

        lax.fori_loop(begin, end, step, 0)

    def block_copy(phase, buffer, p):
        a, b = OFFSETS[p]
        x = lax.rem(w // 4 + 4 - a, 4)
        z = lax.rem(lax.rem(w, 4) + 4 - b, 4)
        return pltpu.make_async_remote_copy(
            src_ref=buffer.at[0],
            dst_ref=buffer.at[p],
            send_sem=send_b.at[phase, p],
            recv_sem=recv_b.at[phase, p],
            device_id={"wide": x * 4 + z},
            device_id_type=MESH,
        )

    def block_send(phase, buffer):
        for p in range(1, NW):
            block_copy(phase, buffer, p).start()

    def block_arrived(phase, buffer, p):
        pltpu.make_async_remote_copy(
            src_ref=buffer.at[0],
            dst_ref=buffer.at[p],
            send_sem=send_b.at[phase, p],
            recv_sem=recv_b.at[phase, p],
            device_id={"wide": w},
            device_id_type=MESH,
        ).wait_recv()

    def wide_copy(phase, src, dst, target, slot):
        return pltpu.make_async_remote_copy(
            src_ref=src,
            dst_ref=dst.at[slot],
            send_sem=send_w.at[phase, target],
            recv_sem=recv_w.at[phase, slot],
            device_id={"wide": target},
            device_id_type=MESH,
        )

    def narrow_copy(phase, src, dst, target, slot):
        return pltpu.make_async_remote_copy(
            src_ref=src,
            dst_ref=dst.at[slot],
            send_sem=send_n.at[phase, target],
            recv_sem=recv_n.at[phase, slot],
            device_id={"narrow": target},
            device_id_type=MESH,
        )

    def wide_send(phase, dst):
        loop(1, NW, lambda p: wide_copy(phase, dst.at[w], dst, lax.rem(w + p, NW), w).start())

    def wide_recv(phase, dst):
        def one(p):
            s = lax.rem(w + p, NW)
            wide_copy(phase, dst.at[s], dst, s, s).wait_recv()

        loop(1, NW, one)

    def wide_sent(phase, dst):
        def one(p):
            s = lax.rem(w + p, NW)
            wide_copy(phase, dst.at[w], dst, s, w).wait_send()

        loop(1, NW, one)

    def narrow_send(phase, dst, src=None, scatter=None):
        def one(p):
            t = lax.rem(n + p, NN)
            source = dst.at[n] if src is None else src
            narrow_copy(phase, source if scatter is None else scatter.at[t], dst, t, n).start()

        loop(1, NN, one)

    def narrow_recv(phase, dst):
        def one(p):
            s = lax.rem(n + p, NN)
            narrow_copy(phase, dst.at[s], dst, s, s).wait_recv()

        loop(1, NN, one)

    def narrow_sent(phase, dst):
        def one(p):
            s = lax.rem(n + p, NN)
            narrow_copy(phase, dst.at[n], dst, s, n).wait_send()

        loop(1, NN, one)

    def all_of(buffer, count):
        parts = [buffer[i] for i in range(count)]
        while len(parts) > 1:
            parts = [parts[i] + parts[i + 1] for i in range(0, len(parts), 2)]
        return parts[0]

    barrier = pltpu.get_barrier_semaphore()

    def greet_wide(p):
        pl.semaphore_signal(barrier, inc=1, device_id={"wide": lax.rem(w + p, NW)}, device_id_type=MESH)

    def greet_narrow(p):
        pl.semaphore_signal(barrier, inc=1, device_id={"narrow": lax.rem(n + p, NN)}, device_id_type=MESH)

    loop(1, NW, greet_wide)
    loop(1, NN, greet_narrow)
    loads = [
        pltpu.make_async_copy(pos_hbm, cpos.at[0], load_sem.at[0]),
        pltpu.make_async_copy(noise_hbm, xg0.at[0], load_sem.at[1]),
    ]
    for load in loads:
        load.start()
    za[n] = jnp.zeros((S, L), F32)
    for load in loads:
        load.wait()
    rpos[n] = cpos[0]
    pl.semaphore_wait(barrier, NW + NN - 2)

    narrow_send(0, rpos, src=cpos.at[0])
    block_send(0, cpos)
    block_send(1, xg0)
    narrow_recv(0, rpos)

    def build(jb):
        columns = jnp.concatenate([cpos[jb], jnp.zeros((5, L), F32)], axis=0).T
        for c in range(3):
            xjb[c] = jnp.broadcast_to(columns[:, c : c + 1], (L, L))

        def rows_of(ic):
            for half in range(2):
                ib = ic * 2 + half
                xi = [jnp.broadcast_to(rpos[ib, c : c + 1, :], (16, L)) for c in range(3)]
                for jt in range(8):
                    d = [xi[c] - xjb[c, jt * 16 : jt * 16 + 16, :] for c in range(3)]
                    sq = jnp.maximum(d[0] * d[0] + d[1] * d[1] + d[2] * d[2], 1e-20)
                    inv = lax.rsqrt(sq)
                    inv2 = inv * inv
                    near = sq < 4.0
                    iso = jnp.where(near, 1.0 - 0.28125 * (sq * inv), inv * (0.75 + 0.5 * inv2))
                    outer = inv * jnp.where(near, 0.09375, inv2 * (0.75 - 1.5 * inv2))
                    places = pl.ds(pl.multiple_of(jb * L + jt * 16, 16), 16)
                    for k, value in enumerate([outer * d[0], outer * d[1], outer * d[2], iso]):
                        high, low = split(value)
                        lhi[k, ib, places, :] = high
                        llo[k, ib, places, :] = low

        loop(0, NN // 2, rows_of)

    build(0)

    def arrived_build(p):
        block_arrived(0, cpos, p)
        build(p)

    loop(1, NW, arrived_build)

    half_blocks = NW // 2
    depth = half_blocks * L

    def product(phase, xg, out):
        def expand(p):
            lanes = pl.ds(pl.multiple_of(lax.rem(p, half_blocks) * L, L), L)
            half = p // half_blocks
            x = [cpos[p, c : c + 1, :] - CENTRE for c in range(3)]
            v = [xg[p, e] for e in range(3)]
            pieces = [jnp.concatenate([v[e], x[0] * v[e], x[1] * v[e], x[2] * v[e]], axis=0) for e in range(3)]
            pieces.append(jnp.concatenate([jnp.zeros((S, L), F32), -v[0], -v[1], -v[2]], axis=0))
            for k in range(4):
                high, low = split(pieces[k])
                rmat[half, k, 0:64, lanes] = high
                rmat[half, k, 64:128, lanes] = low

        def arrived_expand(p):
            block_arrived(phase, xg, p)
            expand(p)

        acc[...] = jnp.zeros_like(acc)
        accl[...] = jnp.zeros_like(accl)
        expand(0)
        for half in range(2):
            loop(max(1, half * half_blocks), (half + 1) * half_blocks, arrived_expand)
            rows = slice(half * depth, (half + 1) * depth)

            def multiply(k):
                high = jnp.concatenate([lhi[k, ib, rows, :] for ib in range(NN)], axis=1)
                low = jnp.concatenate([llo[k, ib, rows, :] for ib in range(NN)], axis=1)
                acc[...] += jnp.dot(rmat[half, k], high, preferred_element_type=F32)
                accl[...] += jnp.dot(rmat[half, k, 0:64, :], low, preferred_element_type=F32)

            loop(0, 4, multiply)
        for b in range(NN):
            lanes = slice(b * L, b * L + L)
            total = acc[0:64, lanes] + (acc[64:128, lanes] + accl[:, lanes])
            for c in range(3):
                out[b, c] = (rpos[b, c : c + 1, :] - CENTRE) * total[0:16] - total[16 + 16 * c : 32 + 16 * c]

    lane = lax.broadcasted_iota(jnp.int32, (S, L), 1)

    product(1, xg0, pb1)
    rb1[n] = pb1[n]
    narrow_send(1, rb1, scatter=pb1)
    narrow_recv(1, rb1)
    xg1[0] = all_of(rb1, NN)
    block_send(2, xg1)

    part = jnp.zeros((2 * S, L), F32)
    for c in range(3):
        a, b = xg0[0, c], xg1[0, c]
        part = part + mt(jnp.concatenate([a, b], axis=0), jnp.concatenate([a, b, b, b, b, b, b, b], axis=0))
    ga1[n] = jnp.where(lane < 32, part[0:16], part[16:32])
    narrow_send(2, ga1)
    narrow_recv(2, ga1)
    gb1[w] = all_of(ga1, NN)
    wide_send(0, gb1)

    product(2, xg1, pb2)
    rb2[n] = pb2[n]
    narrow_send(3, rb2, scatter=pb2)
    narrow_recv(3, rb2)
    y1 = all_of(rb2, NN)
    xg2[0] = y1
    block_send(3, xg2)
    xr[n] = y1
    narrow_send(4, xr)

    wide_recv(0, gb1)
    total = all_of(gb1, NW)
    g00, g01, g11 = total[:, 0:16], total[:, 16:32], total[:, 32:48]
    upper0, inv0 = cholesky_pair(g00)

    def inside(g):
        return mt(mm(inv0, g), inv0)

    h1, c11, k1 = inside(g01), inside(g00), inside(g11)
    f1 = h1 + (h1 - mm(c11, h1))
    f1t = transposed(f1)
    fh = mm(f1t, h1)
    gram = k1 - fh - transposed(fh) + mm(f1t, mm(c11, f1))
    upper1, inv1 = cholesky_pair(gram)
    p21t = mm(inv1, inv0)
    p20t = -mm(mm(inv1, f1t), inv0)
    part = jnp.zeros((5 * S, L), F32)
    for c in range(3):
        a, y0, y1c = xg0[0, c], xg1[0, c], xg2[0, c]
        q1 = mm(inv0, a)
        q2 = mm(p20t, a) + mm(p21t, y0)
        wv = mm(p20t, y0) + mm(p21t, y1c)
        vec_ref[c, 0:16] = q1
        vec_ref[c, 16:32] = q2
        vec_ref[c, 32:48] = wv
        part = part + mt(
            jnp.concatenate([q1, q2, wv, y0, y1c], axis=0), jnp.concatenate([q1, q2, wv, q2, wv, wv, y1c, y1c], axis=0)
        )
    packed = jnp.where(lane < 48, part[0:16], part[16:32])
    packed = jnp.where(lane < 80, packed, part[32:48])
    packed = jnp.where(lane < 96, packed, part[48:64])
    ga2[n] = jnp.where(lane < 112, packed, part[64:80])
    narrow_send(5, ga2)
    narrow_recv(5, ga2)
    gb2[w] = all_of(ga2, NN)
    wide_send(1, gb2)

    product(3, xg2, pz)
    narrow_recv(4, xr)
    part = jnp.zeros((S, S), F32)
    for c in range(3):
        part = part + mt(
            jnp.concatenate([xr[b, c] for b in range(NN)], axis=1), jnp.concatenate([pz[b, c] for b in range(NN)], axis=1)
        )
    za[n, :, 0:16] = part
    narrow_send(6, za)
    wide_recv(1, gb2)
    total = all_of(gb2, NW)
    narrow_recv(6, za)
    zb[w] = all_of(za, NN)
    wide_send(2, zb)

    c11, c12, ha, c22, hb, k, g12, g22 = [total[:, 16 * i : 16 * i + 16] for i in range(8)]
    p20, p21 = transposed(p20t), transposed(p21t)
    c12t = transposed(c12)
    fa = ha + (ha - mm(c11, ha) - mm(c12, hb))
    fb = hb + (hb - mm(c12t, ha) - mm(c22, hb))
    fat, fbt = transposed(fa), transposed(fb)
    hat, hbt = transposed(ha), transposed(hb)
    fh = mm(fat, ha) + mm(fbt, hb)
    cf = mm(fat, mm(c11, fa) + mm(c12, fb)) + mm(fbt, mm(c12t, fa) + mm(c22, fb))
    upper2, inv2 = cholesky_pair(k - fh - transposed(fh) + cf)
    zz = mm(p20t, mm(g12, p20) + mm(g22, p21)) + mm(p21t, mm(g22, p20))
    wmq1 = mm(hat, f1) + mm(hbt, upper1)
    side = mm(wmq1, fa) + mm(k, fb)
    inner = zz - side - transposed(side) + mm(fat, mm(h1, fa) + mm(ha, fb)) + mm(fbt, mm(hat, fa) + mm(hb, fb))
    a3 = mt(mm(inv2, inner), inv2)

    def sym(value):
        return 0.5 * (value + transposed(value))

    order = 3 * S
    tri = jnp.zeros((order, order), F32)
    low = [
        (lax.broadcasted_iota(jnp.int32, (order, S), 0) == lax.broadcasted_iota(jnp.int32, (order, S), 1) + S * i).astype(F32)
        for i in range(3)
    ]
    blocks = [(0, 0, sym(h1)), (1, 1, sym(hb)), (2, 2, sym(a3)), (1, 0, upper1), (2, 1, upper2)]
    blocks += [(0, 1, transposed(upper1)), (1, 2, transposed(upper2))]
    for i, j, block in blocks:
        tri = tri + mt(mm(low[i], block), low[j])
    tri_ref[...] = tri
    mix_ref[...] = mm(low[2], mm(inv2, p21t))
    low_ref[...] = transposed(upper0)
    for c in range(3):
        q1, q2, wv = vec_ref[c, 0:16], vec_ref[c, 16:32], vec_ref[c, 32:48]
        vec_ref[c, 32:48] = mm(inv2, wv - mm(fat, q1) - mm(fbt, q2))
    wide_recv(2, zb)
    ztot_ref[...] = all_of(zb, NW)

    for phase, buffer in enumerate([cpos, xg0, xg1, xg2]):
        for p in range(1, NW):
            block_copy(phase, buffer, p).wait_send()
    for phase, buffer in enumerate([gb1, gb2, zb]):
        wide_sent(phase, buffer)
    for phase, buffer in enumerate([rpos, rb1, ga1, rb2, xr, ga2, za]):
        narrow_sent(phase, buffer)


def last_kernel(vec_ref, tri_ref, mix_ref, low_ref, ztot_ref, out_ref, y_ref, z_ref):
    zraw = ztot_ref[:, 0:16]
    mix = mix_ref[...]
    tri = tri_ref[...] + mt(mm(mix, 0.5 * (zraw + transposed(zraw))), mix)
    order = 3 * S
    scale = jnp.sqrt(jnp.sum(tri * tri))
    ident = eye(order)
    y_ref[...] = tri / scale
    z_ref[...] = ident

    def more(carry):
        step, gap = carry
        return jnp.logical_and(step < ROOT_STEPS, jnp.logical_not(gap < 1e-8))

    def newton(carry):
        step, _ = carry
        y, z = y_ref[...], z_ref[...]
        zy = mm(z, y)
        factor = 1.5 * ident - 0.5 * zy
        y_ref[...] = mm(y, factor)
        z_ref[...] = mm(factor, z)
        off = zy - ident
        return step + 1, jnp.sum(off * off)

    lax.while_loop(more, newton, (jnp.int32(0), jnp.float32(1.0)))
    root = y_ref[...] * jnp.sqrt(scale)
    first = (
        lax.broadcasted_iota(jnp.int32, (S, order), 0) == lax.broadcasted_iota(jnp.int32, (S, order), 1)
    ).astype(F32)
    mixing = mm(low_ref[...], mt(first, root))
    for c in range(3):
        out_ref[c] = mm(mixing, vec_ref[c])


def per_device(positions, noise):
    block = (3, S, L)
    order = 3 * S
    vmem = pl.BlockSpec(memory_space=pltpu.VMEM)
    middle = pl.pallas_call(
        main_kernel,
        out_shape=[
            jax.ShapeDtypeStruct((3, order, L), F32),
            jax.ShapeDtypeStruct((order, order), F32),
            jax.ShapeDtypeStruct((order, S), F32),
            jax.ShapeDtypeStruct((S, S), F32),
            jax.ShapeDtypeStruct((S, L), F32),
        ],
        in_specs=[pl.BlockSpec(memory_space=pl.ANY)] * 2,
        out_specs=[vmem] * 5,
        scratch_shapes=[
            pltpu.VMEM((NW, 3, L), F32),
            pltpu.VMEM((NN, 3, L), F32),
            pltpu.VMEM((NW, *block), F32),
            pltpu.VMEM((NW, *block), F32),
            pltpu.VMEM((NW, *block), F32),
            pltpu.VMEM((NN, *block), F32),
            pltpu.VMEM((NN, *block), F32),
            pltpu.VMEM((NN, *block), F32),
            pltpu.VMEM((NN, *block), F32),
            pltpu.VMEM((NN, *block), F32),
            pltpu.VMEM((NN, *block), F32),
            pltpu.VMEM((4, NN, NW * L, L), BF16),
            pltpu.VMEM((4, NN, NW * L, L), BF16),
            pltpu.VMEM((2, 4, L, NW * L // 2), BF16),
            pltpu.VMEM((L, NN * L), F32),
            pltpu.VMEM((64, NN * L), F32),
            pltpu.VMEM((3, L, L), F32),
            pltpu.VMEM((NN, S, L), F32),
            pltpu.VMEM((NW, S, L), F32),
            pltpu.VMEM((NN, S, L), F32),
            pltpu.VMEM((NW, S, L), F32),
            pltpu.VMEM((NN, S, L), F32),
            pltpu.VMEM((NW, S, L), F32),
            pltpu.SemaphoreType.DMA((4, NW)),
            pltpu.SemaphoreType.DMA((4, NW)),
            pltpu.SemaphoreType.DMA((3, NW)),
            pltpu.SemaphoreType.DMA((3, NW)),
            pltpu.SemaphoreType.DMA((7, NN)),
            pltpu.SemaphoreType.DMA((7, NN)),
            pltpu.SemaphoreType.DMA((2,)),
        ],
        compiler_params=pltpu.CompilerParams(
            collective_id=0, has_side_effects=True, vmem_limit_bytes=56 * 1024 * 1024
        ),
        name="lanczos",
    )(positions, noise)
    return pl.pallas_call(
        last_kernel,
        out_shape=jax.ShapeDtypeStruct(block, F32),
        in_specs=[vmem] * 5,
        out_specs=vmem,
        scratch_shapes=[pltpu.VMEM((order, order), F32), pltpu.VMEM((order, order), F32)],
        name="finish",
    )(*middle)


def solution(mesh):
    axes = ("wide", "narrow")
    return jax.shard_map(
        per_device,
        mesh=mesh,
        in_specs=(P(None, axes), P(None, None, axes)),
        out_specs=P(None, None, axes),
        check_vma=False,
    )
```

time: 106 us -> 92.9 us (0.88)
  Pallas kernels: 106 us -> 92.7 us
    pallas_call x1, Pallas kernels: 94.7 us -> 85.3 us  [per_device(): pl.pallas_call(main_kernel, out_shape=[jax.ShapeDtypeStruct((3, order, L)...]
    pallas_call x1, Pallas kernels: 11.5 us -> 7.35 us  [per_device(): pl.pallas_call(last_kernel, out_shape=jax.ShapeDtypeStruct(block, F32), i...]
where the time goes in v2:
time: 92.9 us; the launch traced here: 92.7 us
  Pallas kernels  92.7 us (100%)
    pallas_call x1, Pallas kernels, per_device(): pl.pallas_call(main_kernel, out_shape=[jax.ShapeDtypeStruct((3, order, L)...  85.3 us
    pallas_call x1, Pallas kernels, per_device(): pl.pallas_call(last_kernel, out_shape=jax.ShapeDtypeStruct(block, F32), i...  7.35 us

profile of v2, /device:TPU:1, one launch (start us, length us, event | category | flops | bytes accessed | tf_op | source)
XLA Modules:
  0.0 92.7 jit_solution(9930629976793893138)
XLA Ops:
  0.0 85.3 %lanczos.1 = (f32[3,48,128]{2,1,0:T(8,128)}, f32[48,48]{1,0:T(8,128)}, f32[48,16]{1,0:T(8,128)}, f32[16,16]{1,0:T(8,128)}, f32[16,128]{1,0:T(8,128)}) custom-call(f32[3,128]{1,0:T(4,128)} %pos_hbm.1, f32[3,16,128]{2,1,0:T(8,128)} %noise_hbm.1), custom_call_target="tpu_custom_call" | custom-call | tf_op jit(solution)/shard_map/lanczos/pallas_call | solution.py:477
  85.3 7.4 %finish.1 = f32[3,16,128]{2,1,0:T(8,128)} custom-call(f32[3,48,128]{2,1,0:T(8,128)} %get-tuple-element.10.vec_ref, f32[48,48]{1,0:T(8,128)} %get-tuple-element.11.tri_ref, f32[48,16]{1,0:T(8,128)} %get-tuple-element.12.mix_ref, f32[16,16]{1,0:T(8,128)} %get-tuple-element.13.low_ref, f32[16,128]{1,0:T(8,128)} %get-tuple-element.14.ztot_ref), custom_call_target="tpu_custom_call" | custom-call | tf_op jit(solution)/shard_map/finish/pallas_call | solution.py:525

commit v3 on v2

--- a/solution.py
+++ b/solution.py
@@ -65,6 +65,8 @@
 
 
 OFFSETS = sorted([(a, b) for a in range(4) for b in range(4)], key=hops)
+ROWS = [(2, 0), (2, 1), (1, 0), (1, 1), (3, 0), (3, 1), (0, 1), (0, 0)]
+OWN = NN - 1
 
 
 def main_kernel(
@@ -90,7 +92,6 @@
     llo,
     rmat,
     acc,
-    accl,
     xjb,
     ga1,
     gb1,
@@ -104,6 +105,8 @@
     recv_w,
     send_n,
     recv_n,
+    send_q,
+    recv_q,
     load_sem,
 ):
     w = lax.axis_index("wide")
@@ -163,6 +166,19 @@
             device_id_type=MESH,
         )
 
+    def row_copy(phase, src, dst, q, away):
+        a, b = ROWS[q]
+        y = lax.rem(n // 2 + (a if away else 4 - a), 4)
+        core = lax.rem(lax.rem(n, 2) + b, 2)
+        return pltpu.make_async_remote_copy(
+            src_ref=src,
+            dst_ref=dst.at[q],
+            send_sem=send_q.at[phase, q],
+            recv_sem=recv_q.at[phase, q],
+            device_id={"narrow": y * 2 + core},
+            device_id_type=MESH,
+        )
+
     def wide_send(phase, dst):
         loop(1, NW, lambda p: wide_copy(phase, dst.at[w], dst, lax.rem(w + p, NW), w).start())
 
@@ -180,13 +196,8 @@
 
         loop(1, NW, one)
 
-    def narrow_send(phase, dst, src=None, scatter=None):
-        def one(p):
-            t = lax.rem(n + p, NN)
-            source = dst.at[n] if src is None else src
-            narrow_copy(phase, source if scatter is None else scatter.at[t], dst, t, n).start()
-
-        loop(1, NN, one)
+    def narrow_send(phase, dst):
+        loop(1, NN, lambda p: narrow_copy(phase, dst.at[n], dst, lax.rem(n + p, NN), n).start())
 
     def narrow_recv(phase, dst):
         def one(p):
@@ -227,13 +238,15 @@
     za[n] = jnp.zeros((S, L), F32)
     for load in loads:
         load.wait()
-    rpos[n] = cpos[0]
+    rpos[OWN] = cpos[0]
     pl.semaphore_wait(barrier, NW + NN - 2)
 
-    narrow_send(0, rpos, src=cpos.at[0])
+    for q in range(OWN):
+        row_copy(0, cpos.at[0], rpos, q, False).start()
     block_send(0, cpos)
     block_send(1, xg0)
-    narrow_recv(0, rpos)
+    for q in range(OWN):
+        row_copy(0, cpos.at[0], rpos, q, False).wait_recv()
 
     def build(jb):
         columns = jnp.concatenate([cpos[jb], jnp.zeros((5, L), F32)], axis=0).T
@@ -271,7 +284,7 @@
     half_blocks = NW // 2
     depth = half_blocks * L
 
-    def product(phase, xg, out):
+    def product(phase, xg, out, between, emit):
         def expand(p):
             lanes = pl.ds(pl.multiple_of(lax.rem(p, half_blocks) * L, L), L)
             half = p // half_blocks
@@ -288,33 +301,57 @@
             block_arrived(phase, xg, p)
             expand(p)
 
-        acc[...] = jnp.zeros_like(acc)
-        accl[...] = jnp.zeros_like(accl)
+        def pair_of(half, q):
+            rows = slice(half * depth, (half + 1) * depth)
+            total, small = None, None
+            for k in range(4):
+                high = jnp.concatenate([lhi[k, q, rows, :], lhi[k, q + 1, rows, :]], axis=1)
+                low = jnp.concatenate([llo[k, q, rows, :], llo[k, q + 1, rows, :]], axis=1)
+                one = jnp.dot(rmat[half, k], high, preferred_element_type=F32)
+                two = jnp.dot(rmat[half, k, 0:64, :], low, preferred_element_type=F32)
+                total = one if total is None else total + one
+                small = two if small is None else small + two
+            return total[0:64] + (total[64:128] + small)
+
         expand(0)
-        for half in range(2):
-            loop(max(1, half * half_blocks), (half + 1) * half_blocks, arrived_expand)
-            rows = slice(half * depth, (half + 1) * depth)
-
-            def multiply(k):
-                high = jnp.concatenate([lhi[k, ib, rows, :] for ib in range(NN)], axis=1)
-                low = jnp.concatenate([llo[k, ib, rows, :] for ib in range(NN)], axis=1)
-                acc[...] += jnp.dot(rmat[half, k], high, preferred_element_type=F32)
-                accl[...] += jnp.dot(rmat[half, k, 0:64, :], low, preferred_element_type=F32)
-
-            loop(0, 4, multiply)
-        for b in range(NN):
-            lanes = slice(b * L, b * L + L)
-            total = acc[0:64, lanes] + (acc[64:128, lanes] + accl[:, lanes])
-            for c in range(3):
-                out[b, c] = (rpos[b, c : c + 1, :] - CENTRE) * total[0:16] - total[16 + 16 * c : 32 + 16 * c]
+        loop(1, half_blocks, arrived_expand)
+
+        def first(g):
+            value = pair_of(0, g * 2)
+            acc[g * 2] = value[:, 0:L]
+            acc[g * 2 + 1] = value[:, L : 2 * L]
+
+        loop(0, NN // 2, first)
+        between()
+        loop(half_blocks, NW, arrived_expand)
+        for g in range(NN // 2):
+            value = pair_of(1, g * 2)
+            for side in range(2):
+                q = g * 2 + side
+                total = acc[q] + value[:, side * L : side * L + L]
+                for c in range(3):
+                    out[q, c] = (rpos[q, c : c + 1, :] - CENTRE) * total[0:16] - total[16 + 16 * c : 32 + 16 * c]
+                emit(q)
+
+    def nothing(*_):
+        return None
+
+    def scatter(phase, parts, sums):
+        def emit(q):
+            if q != OWN:
+                row_copy(phase, parts.at[q], sums, q, True).start()
+
+        return emit
+
+    def summed(phase, parts, sums):
+        for q in range(OWN):
+            row_copy(phase, parts.at[q], sums, q, True).wait_recv()
+        return ((sums[0] + sums[1]) + (sums[2] + sums[3])) + ((sums[4] + sums[5]) + (sums[6] + parts[OWN]))
 
     lane = lax.broadcasted_iota(jnp.int32, (S, L), 1)
 
-    product(1, xg0, pb1)
-    rb1[n] = pb1[n]
-    narrow_send(1, rb1, scatter=pb1)
-    narrow_recv(1, rb1)
-    xg1[0] = all_of(rb1, NN)
+    product(1, xg0, pb1, nothing, scatter(1, pb1, rb1))
+    xg1[0] = summed(1, pb1, rb1)
     block_send(2, xg1)
 
     part = jnp.zeros((2 * S, L), F32)
@@ -322,20 +359,14 @@
         a, b = xg0[0, c], xg1[0, c]
         part = part + mt(jnp.concatenate([a, b], axis=0), jnp.concatenate([a, b, b, b, b, b, b, b], axis=0))
     ga1[n] = jnp.where(lane < 32, part[0:16], part[16:32])
-    narrow_send(2, ga1)
-    narrow_recv(2, ga1)
-    gb1[w] = all_of(ga1, NN)
-    wide_send(0, gb1)
-
-    product(2, xg1, pb2)
-    rb2[n] = pb2[n]
-    narrow_send(3, rb2, scatter=pb2)
-    narrow_recv(3, rb2)
-    y1 = all_of(rb2, NN)
-    xg2[0] = y1
-    block_send(3, xg2)
-    xr[n] = y1
-    narrow_send(4, xr)
+    narrow_send(0, ga1)
+
+    def forward1():
+        narrow_recv(0, ga1)
+        gb1[w] = all_of(ga1, NN)
+        wide_send(0, gb1)
+
+    product(2, xg1, pb2, forward1, scatter(2, pb2, rb2))
 
     wide_recv(0, gb1)
     total = all_of(gb1, NW)
@@ -353,14 +384,24 @@
     upper1, inv1 = cholesky_pair(gram)
     p21t = mm(inv1, inv0)
     p20t = -mm(mm(inv1, f1t), inv0)
+    for c in range(3):
+        a, y0 = xg0[0, c], xg1[0, c]
+        vec_ref[c, 0:16] = mm(inv0, a)
+        vec_ref[c, 16:32] = mm(p20t, a) + mm(p21t, y0)
+        vec_ref[c, 32:48] = mm(p20t, y0)
+
+    y1 = summed(2, pb2, rb2)
+    xg2[0] = y1
+    block_send(3, xg2)
+    xr[OWN] = y1
+    for q in range(OWN):
+        row_copy(3, xr.at[OWN], xr, q, False).start()
+
     part = jnp.zeros((5 * S, L), F32)
     for c in range(3):
-        a, y0, y1c = xg0[0, c], xg1[0, c], xg2[0, c]
-        q1 = mm(inv0, a)
-        q2 = mm(p20t, a) + mm(p21t, y0)
-        wv = mm(p20t, y0) + mm(p21t, y1c)
-        vec_ref[c, 0:16] = q1
-        vec_ref[c, 16:32] = q2
+        y0, y1c = xg1[0, c], xg2[0, c]
+        q1, q2 = vec_ref[c, 0:16], vec_ref[c, 16:32]
+        wv = vec_ref[c, 32:48] + mm(p21t, y1c)
         vec_ref[c, 32:48] = wv
         part = part + mt(
             jnp.concatenate([q1, q2, wv, y0, y1c], axis=0), jnp.concatenate([q1, q2, wv, q2, wv, wv, y1c, y1c], axis=0)
@@ -369,26 +410,26 @@
     packed = jnp.where(lane < 80, packed, part[32:48])
     packed = jnp.where(lane < 96, packed, part[48:64])
     ga2[n] = jnp.where(lane < 112, packed, part[64:80])
-    narrow_send(5, ga2)
-    narrow_recv(5, ga2)
-    gb2[w] = all_of(ga2, NN)
-    wide_send(1, gb2)
-
-    product(3, xg2, pz)
-    narrow_recv(4, xr)
+    narrow_send(1, ga2)
+
+    def forward2():
+        narrow_recv(1, ga2)
+        gb2[w] = all_of(ga2, NN)
+        wide_send(1, gb2)
+
+    product(3, xg2, pz, forward2, nothing)
+    for q in range(OWN):
+        row_copy(3, xr.at[OWN], xr, q, False).wait_recv()
     part = jnp.zeros((S, S), F32)
     for c in range(3):
         part = part + mt(
             jnp.concatenate([xr[b, c] for b in range(NN)], axis=1), jnp.concatenate([pz[b, c] for b in range(NN)], axis=1)
         )
     za[n, :, 0:16] = part
-    narrow_send(6, za)
+    narrow_send(2, za)
+
     wide_recv(1, gb2)
     total = all_of(gb2, NW)
-    narrow_recv(6, za)
-    zb[w] = all_of(za, NN)
-    wide_send(2, zb)
-
     c11, c12, ha, c22, hb, k, g12, g22 = [total[:, 16 * i : 16 * i + 16] for i in range(8)]
     p20, p21 = transposed(p20t), transposed(p21t)
     c12t = transposed(c12)
@@ -399,6 +440,9 @@
     fh = mm(fat, ha) + mm(fbt, hb)
     cf = mm(fat, mm(c11, fa) + mm(c12, fb)) + mm(fbt, mm(c12t, fa) + mm(c22, fb))
     upper2, inv2 = cholesky_pair(k - fh - transposed(fh) + cf)
+    narrow_recv(2, za)
+    zb[w] = all_of(za, NN)
+    wide_send(2, zb)
     zz = mm(p20t, mm(g12, p20) + mm(g22, p21)) + mm(p21t, mm(g22, p20))
     wmq1 = mm(hat, f1) + mm(hbt, upper1)
     side = mm(wmq1, fa) + mm(k, fb)
@@ -432,8 +476,13 @@
             block_copy(phase, buffer, p).wait_send()
     for phase, buffer in enumerate([gb1, gb2, zb]):
         wide_sent(phase, buffer)
-    for phase, buffer in enumerate([rpos, rb1, ga1, rb2, xr, ga2, za]):
+    for phase, buffer in enumerate([ga1, ga2, za]):
         narrow_sent(phase, buffer)
+    for q in range(OWN):
+        row_copy(0, cpos.at[0], rpos, q, False).wait_send()
+        row_copy(1, pb1.at[q], rb1, q, True).wait_send()
+        row_copy(2, pb2.at[q], rb2, q, True).wait_send()
+        row_copy(3, xr.at[OWN], xr, q, False).wait_send()
 
 
 def last_kernel(vec_ref, tri_ref, mix_ref, low_ref, ztot_ref, out_ref, y_ref, z_ref):
@@ -500,8 +549,7 @@
             pltpu.VMEM((4, NN, NW * L, L), BF16),
             pltpu.VMEM((4, NN, NW * L, L), BF16),
             pltpu.VMEM((2, 4, L, NW * L // 2), BF16),
-            pltpu.VMEM((L, NN * L), F32),
-            pltpu.VMEM((64, NN * L), F32),
+            pltpu.VMEM((NN, 64, L), F32),
             pltpu.VMEM((3, L, L), F32),
             pltpu.VMEM((NN, S, L), F32),
             pltpu.VMEM((NW, S, L), F32),
@@ -513,8 +561,10 @@
             pltpu.SemaphoreType.DMA((4, NW)),
             pltpu.SemaphoreType.DMA((3, NW)),
             pltpu.SemaphoreType.DMA((3, NW)),
-            pltpu.SemaphoreType.DMA((7, NN)),
-            pltpu.SemaphoreType.DMA((7, NN)),
+            pltpu.SemaphoreType.DMA((3, NN)),
+            pltpu.SemaphoreType.DMA((3, NN)),
+            pltpu.SemaphoreType.DMA((4, NN)),
+            pltpu.SemaphoreType.DMA((4, NN)),
             pltpu.SemaphoreType.DMA((2,)),
         ],
         compiler_params=pltpu.CompilerParams(

time: 92.9 us -> 89.5 us (0.963)
  Pallas kernels: 92.7 us -> 89.3 us
    pallas_call x1, Pallas kernels: 85.3 us -> 81.9 us  [per_device(): pl.pallas_call(main_kernel, out_shape=[jax.ShapeDtypeStruct((3, order, L)...]
where the time goes in v3:
time: 89.5 us; the launch traced here: 89.3 us
  Pallas kernels  89.3 us (100%)
    pallas_call x1, Pallas kernels, per_device(): pl.pallas_call(main_kernel, out_shape=[jax.ShapeDtypeStruct((3, order, L)...  81.9 us
    pallas_call x1, Pallas kernels, per_device(): pl.pallas_call(last_kernel, out_shape=jax.ShapeDtypeStruct(block, F32), i...  7.35 us

profile of v3, /device:TPU:1, one launch (start us, length us, event | category | flops | bytes accessed | tf_op | source)
XLA Modules:
  0.0 89.3 jit_solution(15262673017273831724)
XLA Ops:
  0.0 81.9 %lanczos.1 = (f32[3,48,128]{2,1,0:T(8,128)}, f32[48,48]{1,0:T(8,128)}, f32[48,16]{1,0:T(8,128)}, f32[16,16]{1,0:T(8,128)}, f32[16,128]{1,0:T(8,128)}) custom-call(f32[3,128]{1,0:T(4,128)} %pos_hbm.1, f32[3,16,128]{2,1,0:T(8,128)} %noise_hbm.1), custom_call_target="tpu_custom_call" | custom-call | tf_op jit(solution)/shard_map/lanczos/pallas_call | solution.py:526
  81.9 7.4 %finish.1 = f32[3,16,128]{2,1,0:T(8,128)} custom-call(f32[3,48,128]{2,1,0:T(8,128)} %get-tuple-element.10.vec_ref, f32[48,48]{1,0:T(8,128)} %get-tuple-element.11.tri_ref, f32[48,16]{1,0:T(8,128)} %get-tuple-element.12.mix_ref, f32[16,16]{1,0:T(8,128)} %get-tuple-element.13.low_ref, f32[16,128]{1,0:T(8,128)} %get-tuple-element.14.ztot_ref), custom_call_target="tpu_custom_call" | custom-call | tf_op jit(solution)/shard_map/finish/pallas_call | solution.py:575

commit v4 on v3

--- a/solution.py
+++ b/solution.py
@@ -65,8 +65,12 @@
 
 
 OFFSETS = sorted([(a, b) for a in range(4) for b in range(4)], key=hops)
-ROWS = [(2, 0), (2, 1), (1, 0), (1, 1), (3, 0), (3, 1), (0, 1), (0, 0)]
 OWN = NN - 1
+
+
+def row_place(q):
+    g, side = q // 2, q % 2
+    return (2 + g * (g + 1) // 2) % 4, (side + g // 3) % 2
 
 
 def main_kernel(
@@ -167,7 +171,7 @@
         )
 
     def row_copy(phase, src, dst, q, away):
-        a, b = ROWS[q]
+        a, b = row_place(q)
         y = lax.rem(n // 2 + (a if away else 4 - a), 4)
         core = lax.rem(lax.rem(n, 2) + b, 2)
         return pltpu.make_async_remote_copy(
@@ -248,43 +252,46 @@
     for q in range(OWN):
         row_copy(0, cpos.at[0], rpos, q, False).wait_recv()
 
-    def build(jb):
-        columns = jnp.concatenate([cpos[jb], jnp.zeros((5, L), F32)], axis=0).T
-        for c in range(3):
-            xjb[c] = jnp.broadcast_to(columns[:, c : c + 1], (L, L))
-
-        def rows_of(ic):
+    def build(group):
+        for i in range(4):
+            columns = jnp.concatenate([cpos[group * 4 + i], jnp.zeros((5, L), F32)], axis=0).T
+            for c in range(3):
+                xjb[i, c] = jnp.broadcast_to(columns[:, c : c + 1], (L, L))
+
+        def one(step):
+            i = step // 4
             for half in range(2):
-                ib = ic * 2 + half
+                ib = lax.rem(step, 4) * 2 + half
                 xi = [jnp.broadcast_to(rpos[ib, c : c + 1, :], (16, L)) for c in range(3)]
                 for jt in range(8):
-                    d = [xi[c] - xjb[c, jt * 16 : jt * 16 + 16, :] for c in range(3)]
+                    d = [xi[c] - xjb[i, c, jt * 16 : jt * 16 + 16, :] for c in range(3)]
                     sq = jnp.maximum(d[0] * d[0] + d[1] * d[1] + d[2] * d[2], 1e-20)
                     inv = lax.rsqrt(sq)
                     inv2 = inv * inv
                     near = sq < 4.0
                     iso = jnp.where(near, 1.0 - 0.28125 * (sq * inv), inv * (0.75 + 0.5 * inv2))
                     outer = inv * jnp.where(near, 0.09375, inv2 * (0.75 - 1.5 * inv2))
-                    places = pl.ds(pl.multiple_of(jb * L + jt * 16, 16), 16)
+                    places = pl.ds(pl.multiple_of((group * 4 + i) * L + jt * 16, 16), 16)
                     for k, value in enumerate([outer * d[0], outer * d[1], outer * d[2], iso]):
                         high, low = split(value)
                         lhi[k, ib, places, :] = high
                         llo[k, ib, places, :] = low
 
-        loop(0, NN // 2, rows_of)
-
-    build(0)
-
-    def arrived_build(p):
-        block_arrived(0, cpos, p)
-        build(p)
-
-    loop(1, NW, arrived_build)
+        loop(0, 16, one)
+
+    def arrived_build(group):
+        def arrived(p):
+            block_arrived(0, cpos, p)
+
+        loop(jnp.maximum(group * 4, 1), group * 4 + 4, arrived)
+        build(group)
+
+    loop(0, 4, arrived_build)
 
     half_blocks = NW // 2
     depth = half_blocks * L
 
-    def product(phase, xg, out, between, emit):
+    def product(phase, xg, out, early, between, emit):
         def expand(p):
             lanes = pl.ds(pl.multiple_of(lax.rem(p, half_blocks) * L, L), L)
             half = p // half_blocks
@@ -321,25 +328,33 @@
             acc[g * 2] = value[:, 0:L]
             acc[g * 2 + 1] = value[:, L : 2 * L]
 
-        loop(0, NN // 2, first)
+        loop(0, NN // 4, first)
+        early()
+        loop(NN // 4, NN // 2, first)
         between()
         loop(half_blocks, NW, arrived_expand)
-        for g in range(NN // 2):
+
+        def second(g):
             value = pair_of(1, g * 2)
             for side in range(2):
                 q = g * 2 + side
                 total = acc[q] + value[:, side * L : side * L + L]
                 for c in range(3):
-                    out[q, c] = (rpos[q, c : c + 1, :] - CENTRE) * total[0:16] - total[16 + 16 * c : 32 + 16 * c]
-                emit(q)
+                    out[q, c] = (rpos[q, pl.ds(c, 1), :] - CENTRE) * total[0:16] - total[16 + 16 * c : 32 + 16 * c]
+            emit(g * 2)
+
+        loop(0, NN // 2, second)
 
     def nothing(*_):
         return None
 
     def scatter(phase, parts, sums):
         def emit(q):
-            if q != OWN:
-                row_copy(phase, parts.at[q], sums, q, True).start()
+            row_copy(phase, parts.at[q], sums, q, True).start()
+
+            @pl.when(q + 1 < OWN)
+            def _():
+                row_copy(phase, parts.at[q + 1], sums, q + 1, True).start()
 
         return emit
 
@@ -350,7 +365,7 @@
 
     lane = lax.broadcasted_iota(jnp.int32, (S, L), 1)
 
-    product(1, xg0, pb1, nothing, scatter(1, pb1, rb1))
+    product(1, xg0, pb1, nothing, nothing, scatter(1, pb1, rb1))
     xg1[0] = summed(1, pb1, rb1)
     block_send(2, xg1)
 
@@ -366,7 +381,7 @@
         gb1[w] = all_of(ga1, NN)
         wide_send(0, gb1)
 
-    product(2, xg1, pb2, forward1, scatter(2, pb2, rb2))
+    product(2, xg1, pb2, forward1, nothing, scatter(2, pb2, rb2))
 
     wide_recv(0, gb1)
     total = all_of(gb1, NW)
@@ -381,6 +396,13 @@
     f1t = transposed(f1)
     fh = mm(f1t, h1)
     gram = k1 - fh - transposed(fh) + mm(f1t, mm(c11, f1))
+    y1 = summed(2, pb2, rb2)
+    xg2[0] = y1
+    block_send(3, xg2)
+    xr[OWN] = y1
+    for q in range(OWN):
+        row_copy(3, xr.at[OWN], xr, q, False).start()
+
     upper1, inv1 = cholesky_pair(gram)
     p21t = mm(inv1, inv0)
     p20t = -mm(mm(inv1, f1t), inv0)
@@ -389,13 +411,6 @@
         vec_ref[c, 0:16] = mm(inv0, a)
         vec_ref[c, 16:32] = mm(p20t, a) + mm(p21t, y0)
         vec_ref[c, 32:48] = mm(p20t, y0)
-
-    y1 = summed(2, pb2, rb2)
-    xg2[0] = y1
-    block_send(3, xg2)
-    xr[OWN] = y1
-    for q in range(OWN):
-        row_copy(3, xr.at[OWN], xr, q, False).start()
 
     part = jnp.zeros((5 * S, L), F32)
     for c in range(3):
@@ -417,7 +432,7 @@
         gb2[w] = all_of(ga2, NN)
         wide_send(1, gb2)
 
-    product(3, xg2, pz, forward2, nothing)
+    product(3, xg2, pz, nothing, forward2, nothing)
     for q in range(OWN):
         row_copy(3, xr.at[OWN], xr, q, False).wait_recv()
     part = jnp.zeros((S, S), F32)
@@ -550,7 +565,7 @@
             pltpu.VMEM((4, NN, NW * L, L), BF16),
             pltpu.VMEM((2, 4, L, NW * L // 2), BF16),
             pltpu.VMEM((NN, 64, L), F32),
-            pltpu.VMEM((3, L, L), F32),
+            pltpu.VMEM((4, 3, L, L), F32),
             pltpu.VMEM((NN, S, L), F32),
             pltpu.VMEM((NW, S, L), F32),
             pltpu.VMEM((NN, S, L), F32),

time: 89.5 us -> 86.8 us (0.970)
  Pallas kernels: 89.3 us -> 86.6 us
    pallas_call x1, Pallas kernels: 81.9 us -> 79.2 us  [per_device(): pl.pallas_call(main_kernel, out_shape=[jax.ShapeDtypeStruct((3, order, L)...]
where the time goes in v4:
time: 86.8 us; the launch traced here: 86.6 us
  Pallas kernels  86.6 us (100%)
    pallas_call x1, Pallas kernels, per_device(): pl.pallas_call(main_kernel, out_shape=[jax.ShapeDtypeStruct((3, order, L)...  79.2 us
    pallas_call x1, Pallas kernels, per_device(): pl.pallas_call(last_kernel, out_shape=jax.ShapeDtypeStruct(block, F32), i...  7.35 us

profile of v4, /device:TPU:1, one launch (start us, length us, event | category | flops | bytes accessed | tf_op | source)
XLA Modules:
  0.0 86.6 jit_solution(11725955576917191212)
XLA Ops:
  0.0 79.2 %lanczos.1 = (f32[3,48,128]{2,1,0:T(8,128)}, f32[48,48]{1,0:T(8,128)}, f32[48,16]{1,0:T(8,128)}, f32[16,16]{1,0:T(8,128)}, f32[16,128]{1,0:T(8,128)}) custom-call(f32[3,128]{1,0:T(4,128)} %pos_hbm.1, f32[3,16,128]{2,1,0:T(8,128)} %noise_hbm.1), custom_call_target="tpu_custom_call" | custom-call | tf_op jit(solution)/shard_map/lanczos/pallas_call | solution.py:541
  79.2 7.4 %finish.1 = f32[3,16,128]{2,1,0:T(8,128)} custom-call(f32[3,48,128]{2,1,0:T(8,128)} %get-tuple-element.10.vec_ref, f32[48,48]{1,0:T(8,128)} %get-tuple-element.11.tri_ref, f32[48,16]{1,0:T(8,128)} %get-tuple-element.12.mix_ref, f32[16,16]{1,0:T(8,128)} %get-tuple-element.13.low_ref, f32[16,128]{1,0:T(8,128)} %get-tuple-element.14.ztot_ref), custom_call_target="tpu_custom_call" | custom-call | tf_op jit(solution)/shard_map/finish/pallas_call | solution.py:590

commit v5 on v4

--- a/solution.py
+++ b/solution.py
@@ -226,12 +226,15 @@
     barrier = pltpu.get_barrier_semaphore()
 
     def greet_wide(p):
-        pl.semaphore_signal(barrier, inc=1, device_id={"wide": lax.rem(w + p, NW)}, device_id_type=MESH)
+        along_x = lax.rem(w // 4 + p, 4) * 4 + lax.rem(w, 4)
+        along_z = w // 4 * 4 + lax.rem(lax.rem(w, 4) + p, 4)
+        pl.semaphore_signal(barrier, inc=1, device_id={"wide": along_x}, device_id_type=MESH)
+        pl.semaphore_signal(barrier, inc=1, device_id={"wide": along_z}, device_id_type=MESH)
 
     def greet_narrow(p):
         pl.semaphore_signal(barrier, inc=1, device_id={"narrow": lax.rem(n + p, NN)}, device_id_type=MESH)
 
-    loop(1, NW, greet_wide)
+    loop(1, 4, greet_wide)
     loop(1, NN, greet_narrow)
     loads = [
         pltpu.make_async_copy(pos_hbm, cpos.at[0], load_sem.at[0]),
@@ -243,12 +246,28 @@
     for load in loads:
         load.wait()
     rpos[OWN] = cpos[0]
-    pl.semaphore_wait(barrier, NW + NN - 2)
+    pl.semaphore_wait(barrier, 6 + NN - 1)
 
     for q in range(OWN):
         row_copy(0, cpos.at[0], rpos, q, False).start()
-    block_send(0, cpos)
-    block_send(1, xg0)
+    for a in range(1, 4):
+        block_copy(0, cpos, OFFSETS.index((a, 0))).start()
+        block_copy(0, cpos, OFFSETS.index((0, a))).start()
+    for a in range(1, 4):
+        held = OFFSETS.index((a, 0))
+        block_arrived(0, cpos, held)
+        for b in range(1, 4):
+            slot = OFFSETS.index((a, b))
+            pltpu.make_async_remote_copy(
+                src_ref=cpos.at[held],
+                dst_ref=cpos.at[slot],
+                send_sem=send_b.at[0, slot],
+                recv_sem=recv_b.at[0, slot],
+                device_id={"wide": w // 4 * 4 + lax.rem(lax.rem(w, 4) + 4 - b, 4)},
+                device_id_type=MESH,
+            ).start()
+    for a in range(1, 4):
+        block_arrived(0, cpos, OFFSETS.index((0, a)))
     for q in range(OWN):
         row_copy(0, cpos.at[0], rpos, q, False).wait_recv()
 
@@ -279,14 +298,12 @@
 
         loop(0, 16, one)
 
-    def arrived_build(group):
-        def arrived(p):
-            block_arrived(0, cpos, p)
-
-        loop(jnp.maximum(group * 4, 1), group * 4 + 4, arrived)
-        build(group)
-
-    loop(0, 4, arrived_build)
+    build(0)
+    for a in range(1, 4):
+        for b in range(1, 4):
+            block_arrived(0, cpos, OFFSETS.index((a, b)))
+    block_send(1, xg0)
+    loop(1, 4, build)
 
     half_blocks = NW // 2
     depth = half_blocks * L

time: 86.8 us -> 85.8 us (0.988)
  Pallas kernels: 86.6 us -> 85.5 us
    pallas_call x1, Pallas kernels: 79.2 us -> 78.2 us  [per_device(): pl.pallas_call(main_kernel, out_shape=[jax.ShapeDtypeStruct((3, order, L)...]
where the time goes in v5:
time: 85.8 us; the launch traced here: 85.6 us
  Pallas kernels  85.5 us (100%)
    pallas_call x1, Pallas kernels, per_device(): pl.pallas_call(main_kernel, out_shape=[jax.ShapeDtypeStruct((3, order, L)...  78.2 us
    pallas_call x1, Pallas kernels, per_device(): pl.pallas_call(last_kernel, out_shape=jax.ShapeDtypeStruct(block, F32), i...  7.35 us

profile of v5, /device:TPU:1, one launch (start us, length us, event | category | flops | bytes accessed | tf_op | source)
XLA Modules:
  0.0 85.6 jit_solution(9573014118810018990)
XLA Ops:
  0.0 78.2 %lanczos.1 = (f32[3,48,128]{2,1,0:T(8,128)}, f32[48,48]{1,0:T(8,128)}, f32[48,16]{1,0:T(8,128)}, f32[16,16]{1,0:T(8,128)}, f32[16,128]{1,0:T(8,128)}) custom-call(f32[3,128]{1,0:T(4,128)} %pos_hbm.1, f32[3,16,128]{2,1,0:T(8,128)} %noise_hbm.1), custom_call_target="tpu_custom_call" | custom-call | tf_op jit(solution)/shard_map/lanczos/pallas_call | solution.py:558
  78.2 7.4 %finish.1 = f32[3,16,128]{2,1,0:T(8,128)} custom-call(f32[3,48,128]{2,1,0:T(8,128)} %get-tuple-element.10.vec_ref, f32[48,48]{1,0:T(8,128)} %get-tuple-element.11.tri_ref, f32[48,16]{1,0:T(8,128)} %get-tuple-element.12.mix_ref, f32[16,16]{1,0:T(8,128)} %get-tuple-element.13.low_ref, f32[16,128]{1,0:T(8,128)} %get-tuple-element.14.ztot_ref), custom_call_target="tpu_custom_call" | custom-call | tf_op jit(solution)/shard_map/finish/pallas_call | solution.py:607

commit v6 on v5

--- a/solution.py
+++ b/solution.py
@@ -60,11 +60,9 @@
     return high, low
 
 
-def hops(offset):
-    return sum(min(part, 4 - part) for part in offset)
-
-
-OFFSETS = sorted([(a, b) for a in range(4) for b in range(4)], key=hops)
+OFFSETS = [(0, 0), (2, 0), (1, 0), (0, 1), (1, 1), (1, 3), (2, 1), (1, 2), (0, 2), (2, 2)]
+OFFSETS += [(0, 3), (3, 0), (3, 1), (3, 3), (2, 3), (3, 2)]
+HALF = 10
 OWN = NN - 1
 
 
@@ -136,8 +134,8 @@
             device_id_type=MESH,
         )
 
-    def block_send(phase, buffer):
-        for p in range(1, NW):
+    def block_send(phase, buffer, count=NW):
+        for p in range(1, count):
             block_copy(phase, buffer, p).start()
 
     def block_arrived(phase, buffer, p):
@@ -308,12 +306,12 @@
     half_blocks = NW // 2
     depth = half_blocks * L
 
-    def product(phase, xg, out, early, between, emit):
-        def expand(p):
+    def product(phase, xg, out, early, between, emit, symmetric=False):
+        def expand(p, factor=None):
             lanes = pl.ds(pl.multiple_of(lax.rem(p, half_blocks) * L, L), L)
             half = p // half_blocks
             x = [cpos[p, c : c + 1, :] - CENTRE for c in range(3)]
-            v = [xg[p, e] for e in range(3)]
+            v = [xg[p, e] if factor is None else factor * xg[p, e] for e in range(3)]
             pieces = [jnp.concatenate([v[e], x[0] * v[e], x[1] * v[e], x[2] * v[e]], axis=0) for e in range(3)]
             pieces.append(jnp.concatenate([jnp.zeros((S, L), F32), -v[0], -v[1], -v[2]], axis=0))
             for k in range(4):
@@ -325,20 +323,28 @@
             block_arrived(phase, xg, p)
             expand(p)
 
+        def arrived_double(p):
+            block_arrived(phase, xg, p)
+            expand(p, 2.0)
+
+        columns = HALF if symmetric else NW
+
         def pair_of(half, q):
-            rows = slice(half * depth, (half + 1) * depth)
+            size = min(depth, columns * L - half * depth)
+            rows = slice(half * depth, half * depth + size)
             total, small = None, None
             for k in range(4):
                 high = jnp.concatenate([lhi[k, q, rows, :], lhi[k, q + 1, rows, :]], axis=1)
                 low = jnp.concatenate([llo[k, q, rows, :], llo[k, q + 1, rows, :]], axis=1)
-                one = jnp.dot(rmat[half, k], high, preferred_element_type=F32)
-                two = jnp.dot(rmat[half, k, 0:64, :], low, preferred_element_type=F32)
+                one = jnp.dot(rmat[half, k, :, 0:size], high, preferred_element_type=F32)
+                two = jnp.dot(rmat[half, k, 0:64, 0:size], low, preferred_element_type=F32)
                 total = one if total is None else total + one
                 small = two if small is None else small + two
             return total[0:64] + (total[64:128] + small)
 
         expand(0)
-        loop(1, half_blocks, arrived_expand)
+        loop(1, 2, arrived_expand)
+        loop(2, half_blocks, arrived_double if symmetric else arrived_expand)
 
         def first(g):
             value = pair_of(0, g * 2)
@@ -349,7 +355,7 @@
         early()
         loop(NN // 4, NN // 2, first)
         between()
-        loop(half_blocks, NW, arrived_expand)
+        loop(half_blocks, columns, arrived_expand)
 
         def second(g):
             value = pair_of(1, g * 2)
@@ -415,7 +421,7 @@
     gram = k1 - fh - transposed(fh) + mm(f1t, mm(c11, f1))
     y1 = summed(2, pb2, rb2)
     xg2[0] = y1
-    block_send(3, xg2)
+    block_send(3, xg2, HALF)
     xr[OWN] = y1
     for q in range(OWN):
         row_copy(3, xr.at[OWN], xr, q, False).start()
@@ -449,7 +455,7 @@
         gb2[w] = all_of(ga2, NN)
         wide_send(1, gb2)
 
-    product(3, xg2, pz, nothing, forward2, nothing)
+    product(3, xg2, pz, nothing, forward2, nothing, True)
     for q in range(OWN):
         row_copy(3, xr.at[OWN], xr, q, False).wait_recv()
     part = jnp.zeros((S, S), F32)
@@ -459,6 +465,10 @@
         )
     za[n, :, 0:16] = part
     narrow_send(2, za)
+
+    narrow_recv(2, za)
+    zb[w] = all_of(za, NN)
+    wide_send(2, zb)
 
     wide_recv(1, gb2)
     total = all_of(gb2, NW)
@@ -472,9 +482,6 @@
     fh = mm(fat, ha) + mm(fbt, hb)
     cf = mm(fat, mm(c11, fa) + mm(c12, fb)) + mm(fbt, mm(c12t, fa) + mm(c22, fb))
     upper2, inv2 = cholesky_pair(k - fh - transposed(fh) + cf)
-    narrow_recv(2, za)
-    zb[w] = all_of(za, NN)
-    wide_send(2, zb)
     zz = mm(p20t, mm(g12, p20) + mm(g22, p21)) + mm(p21t, mm(g22, p20))
     wmq1 = mm(hat, f1) + mm(hbt, upper1)
     side = mm(wmq1, fa) + mm(k, fb)
@@ -504,7 +511,7 @@
     ztot_ref[...] = all_of(zb, NW)
 
     for phase, buffer in enumerate([cpos, xg0, xg1, xg2]):
-        for p in range(1, NW):
+        for p in range(1, NW if phase < 3 else HALF):
             block_copy(phase, buffer, p).wait_send()
     for phase, buffer in enumerate([gb1, gb2, zb]):
         wide_sent(phase, buffer)

time: 85.8 us -> 85.5 us (level)
  no operation moved by 1% of the time
where the time goes in v6:
time: 85.5 us; the launch traced here: 85.3 us
  Pallas kernels  85.3 us (100%)
    pallas_call x1, Pallas kernels, per_device(): pl.pallas_call(main_kernel, out_shape=[jax.ShapeDtypeStruct((3, order, L)...  77.9 us
    pallas_call x1, Pallas kernels, per_device(): pl.pallas_call(last_kernel, out_shape=jax.ShapeDtypeStruct(block, F32), i...  7.35 us

profile of v6, /device:TPU:1, one launch (start us, length us, event | category | flops | bytes accessed | tf_op | source)
XLA Modules:
  0.0 85.3 jit_solution(17541589660636351823)
XLA Ops:
  0.0 77.9 %lanczos.1 = (f32[3,48,128]{2,1,0:T(8,128)}, f32[48,48]{1,0:T(8,128)}, f32[48,16]{1,0:T(8,128)}, f32[16,16]{1,0:T(8,128)}, f32[16,128]{1,0:T(8,128)}) custom-call(f32[3,128]{1,0:T(4,128)} %pos_hbm.1, f32[3,16,128]{2,1,0:T(8,128)} %noise_hbm.1), custom_call_target="tpu_custom_call" | custom-call | tf_op jit(solution)/shard_map/lanczos/pallas_call | solution.py:565
  77.9 7.4 %finish.1 = f32[3,16,128]{2,1,0:T(8,128)} custom-call(f32[3,48,128]{2,1,0:T(8,128)} %get-tuple-element.10.vec_ref, f32[48,48]{1,0:T(8,128)} %get-tuple-element.11.tri_ref, f32[48,16]{1,0:T(8,128)} %get-tuple-element.12.mix_ref, f32[16,16]{1,0:T(8,128)} %get-tuple-element.13.low_ref, f32[16,128]{1,0:T(8,128)} %get-tuple-element.14.ztot_ref), custom_call_target="tpu_custom_call" | custom-call | tf_op jit(solution)/shard_map/finish/pallas_call | solution.py:614

commit v7 on v6

--- a/solution.py
+++ b/solution.py
@@ -329,13 +329,13 @@
 
         columns = HALF if symmetric else NW
 
-        def pair_of(half, q):
+        def pair_of(half, q, count=2):
             size = min(depth, columns * L - half * depth)
             rows = slice(half * depth, half * depth + size)
             total, small = None, None
             for k in range(4):
-                high = jnp.concatenate([lhi[k, q, rows, :], lhi[k, q + 1, rows, :]], axis=1)
-                low = jnp.concatenate([llo[k, q, rows, :], llo[k, q + 1, rows, :]], axis=1)
+                high = jnp.concatenate([lhi[k, q + i, rows, :] for i in range(count)], axis=1)
+                low = jnp.concatenate([llo[k, q + i, rows, :] for i in range(count)], axis=1)
                 one = jnp.dot(rmat[half, k, :, 0:size], high, preferred_element_type=F32)
                 two = jnp.dot(rmat[half, k, 0:64, 0:size], low, preferred_element_type=F32)
                 total = one if total is None else total + one
@@ -347,13 +347,18 @@
         loop(2, half_blocks, arrived_double if symmetric else arrived_expand)
 
         def first(g):
-            value = pair_of(0, g * 2)
-            acc[g * 2] = value[:, 0:L]
-            acc[g * 2 + 1] = value[:, L : 2 * L]
-
-        loop(0, NN // 4, first)
-        early()
-        loop(NN // 4, NN // 2, first)
+            value = pair_of(0, g * 4, 4)
+            for side in range(4):
+                acc[g * 4 + side] = value[:, side * L : side * L + L]
+
+        def turn(g):
+            first(g)
+
+            @pl.when(g == 0)
+            def _():
+                early()
+
+        loop(0, NN // 4, turn)
         between()
         loop(half_blocks, columns, arrived_expand)
 

time: 85.5 us -> 84.7 us (level)
  no operation moved by 1% of the time
where the time goes in v7:
time: 84.7 us; the launch traced here: 84.5 us
  Pallas kernels  84.5 us (100%)
    pallas_call x1, Pallas kernels, per_device(): pl.pallas_call(main_kernel, out_shape=[jax.ShapeDtypeStruct((3, order, L)...  77.2 us
    pallas_call x1, Pallas kernels, per_device(): pl.pallas_call(last_kernel, out_shape=jax.ShapeDtypeStruct(block, F32), i...  7.35 us

profile of v7, /device:TPU:1, one launch (start us, length us, event | category | flops | bytes accessed | tf_op | source)
XLA Modules:
  0.0 84.5 jit_solution(3125291655032801369)
XLA Ops:
  0.0 77.2 %lanczos.1 = (f32[3,48,128]{2,1,0:T(8,128)}, f32[48,48]{1,0:T(8,128)}, f32[48,16]{1,0:T(8,128)}, f32[16,16]{1,0:T(8,128)}, f32[16,128]{1,0:T(8,128)}) custom-call(f32[3,128]{1,0:T(4,128)} %pos_hbm.1, f32[3,16,128]{2,1,0:T(8,128)} %noise_hbm.1), custom_call_target="tpu_custom_call" | custom-call | tf_op jit(solution)/shard_map/lanczos/pallas_call | solution.py:570
  77.2 7.4 %finish.1 = f32[3,16,128]{2,1,0:T(8,128)} custom-call(f32[3,48,128]{2,1,0:T(8,128)} %get-tuple-element.10.vec_ref, f32[48,48]{1,0:T(8,128)} %get-tuple-element.11.tri_ref, f32[48,16]{1,0:T(8,128)} %get-tuple-element.12.mix_ref, f32[16,16]{1,0:T(8,128)} %get-tuple-element.13.low_ref, f32[16,128]{1,0:T(8,128)} %get-tuple-element.14.ztot_ref), custom_call_target="tpu_custom_call" | custom-call | tf_op jit(solution)/shard_map/finish/pallas_call | solution.py:619

commit v8 on v7

--- a/solution.py
+++ b/solution.py
@@ -60,9 +60,10 @@
     return high, low
 
 
-OFFSETS = [(0, 0), (2, 0), (1, 0), (0, 1), (1, 1), (1, 3), (2, 1), (1, 2), (0, 2), (2, 2)]
-OFFSETS += [(0, 3), (3, 0), (3, 1), (3, 3), (2, 3), (3, 2)]
-HALF = 10
+OFFSETS = [(0, 0), (2, 0), (1, 0), (0, 1), (3, 0), (0, 3), (1, 1), (0, 2)]
+OFFSETS += [(1, 3), (2, 1), (1, 2), (2, 2), (3, 3), (3, 1), (2, 3), (3, 2)]
+HALF = (0, 1, 2, 3, 6, 7, 8, 9, 10, 11)
+SELF = (0, 1, 7, 11)
 OWN = NN - 1
 
 
@@ -134,8 +135,8 @@
             device_id_type=MESH,
         )
 
-    def block_send(phase, buffer, count=NW):
-        for p in range(1, count):
+    def block_send(phase, buffer, slots=range(NW)):
+        for p in slots[1:]:
             block_copy(phase, buffer, p).start()
 
     def block_arrived(phase, buffer, p):
@@ -327,24 +328,34 @@
             block_arrived(phase, xg, p)
             expand(p, 2.0)
 
-        columns = HALF if symmetric else NW
-
         def pair_of(half, q, count=2):
-            size = min(depth, columns * L - half * depth)
-            rows = slice(half * depth, half * depth + size)
+            if symmetric:
+                spans = [[(0, 4), (6, 8)], [(0, 4)]][half]
+            else:
+                spans = [(0, half_blocks)]
             total, small = None, None
-            for k in range(4):
+            for k, (begin, end) in [(k, span) for k in range(4) for span in spans]:
+                rows = slice(half * depth + begin * L, half * depth + end * L)
+                places = slice(begin * L, end * L)
                 high = jnp.concatenate([lhi[k, q + i, rows, :] for i in range(count)], axis=1)
                 low = jnp.concatenate([llo[k, q + i, rows, :] for i in range(count)], axis=1)
-                one = jnp.dot(rmat[half, k, :, 0:size], high, preferred_element_type=F32)
-                two = jnp.dot(rmat[half, k, 0:64, 0:size], low, preferred_element_type=F32)
+                one = jnp.dot(rmat[half, k, :, places], high, preferred_element_type=F32)
+                two = jnp.dot(rmat[half, k, 0:64, places], low, preferred_element_type=F32)
                 total = one if total is None else total + one
                 small = two if small is None else small + two
             return total[0:64] + (total[64:128] + small)
 
         expand(0)
-        loop(1, 2, arrived_expand)
-        loop(2, half_blocks, arrived_double if symmetric else arrived_expand)
+        def arrivals(half):
+            begin, end = max(1, half * half_blocks), (half + 1) * half_blocks
+            if not symmetric:
+                loop(begin, end, arrived_expand)
+                return
+            for p in HALF:
+                if begin <= p < end:
+                    (arrived_expand if p in SELF else arrived_double)(p)
+
+        arrivals(0)
 
         def first(g):
             value = pair_of(0, g * 4, 4)
@@ -360,7 +371,7 @@
 
         loop(0, NN // 4, turn)
         between()
-        loop(half_blocks, columns, arrived_expand)
+        arrivals(1)
 
         def second(g):
             value = pair_of(1, g * 2)
@@ -516,7 +527,7 @@
     ztot_ref[...] = all_of(zb, NW)
 
     for phase, buffer in enumerate([cpos, xg0, xg1, xg2]):
-        for p in range(1, NW if phase < 3 else HALF):
+        for p in (HALF[1:] if phase == 3 else range(1, NW)):
             block_copy(phase, buffer, p).wait_send()
     for phase, buffer in enumerate([gb1, gb2, zb]):
         wide_sent(phase, buffer)

time: 84.7 us -> 81.2 us (0.959)
  Pallas kernels: 84.5 us -> 81 us
    pallas_call x1, Pallas kernels: 77.2 us -> 73.6 us  [per_device(): pl.pallas_call(main_kernel, out_shape=[jax.ShapeDtypeStruct((3, order, L)...]
where the time goes in v8:
time: 81.2 us; the launch traced here: 81 us
  Pallas kernels  81 us (100%)
    pallas_call x1, Pallas kernels, per_device(): pl.pallas_call(main_kernel, out_shape=[jax.ShapeDtypeStruct((3, order, L)...  73.6 us
    pallas_call x1, Pallas kernels, per_device(): pl.pallas_call(last_kernel, out_shape=jax.ShapeDtypeStruct(block, F32), i...  7.35 us

profile of v8, /device:TPU:1, one launch (start us, length us, event | category | flops | bytes accessed | tf_op | source)
XLA Modules:
  0.0 81.0 jit_solution(17955785411364767544)
XLA Ops:
  0.0 73.6 %lanczos.1 = (f32[3,48,128]{2,1,0:T(8,128)}, f32[48,48]{1,0:T(8,128)}, f32[48,16]{1,0:T(8,128)}, f32[16,16]{1,0:T(8,128)}, f32[16,128]{1,0:T(8,128)}) custom-call(f32[3,128]{1,0:T(4,128)} %pos_hbm.1, f32[3,16,128]{2,1,0:T(8,128)} %noise_hbm.1), custom_call_target="tpu_custom_call" | custom-call | tf_op jit(solution)/shard_map/lanczos/pallas_call | solution.py:581
  73.6 7.3 %finish.1 = f32[3,16,128]{2,1,0:T(8,128)} custom-call(f32[3,48,128]{2,1,0:T(8,128)} %get-tuple-element.10.vec_ref, f32[48,48]{1,0:T(8,128)} %get-tuple-element.11.tri_ref, f32[48,16]{1,0:T(8,128)} %get-tuple-element.12.mix_ref, f32[16,16]{1,0:T(8,128)} %get-tuple-element.13.low_ref, f32[16,128]{1,0:T(8,128)} %get-tuple-element.14.ztot_ref), custom_call_target="tpu_custom_call" | custom-call | tf_op jit(solution)/shard_map/finish/pallas_call | solution.py:630

commit v9 on v8

--- a/solution.py
+++ b/solution.py
@@ -373,16 +373,19 @@
         between()
         arrivals(1)
 
+        wide = 4 if symmetric else 2
+
         def second(g):
-            value = pair_of(1, g * 2)
-            for side in range(2):
-                q = g * 2 + side
+            value = pair_of(1, g * wide, wide)
+            for side in range(wide):
+                q = g * wide + side
                 total = acc[q] + value[:, side * L : side * L + L]
                 for c in range(3):
                     out[q, c] = (rpos[q, pl.ds(c, 1), :] - CENTRE) * total[0:16] - total[16 + 16 * c : 32 + 16 * c]
-            emit(g * 2)
-
-        loop(0, NN // 2, second)
+            for side in range(0, wide, 2):
+                emit(g * wide + side)
+
+        loop(0, NN // wide, second)
 
     def nothing(*_):
         return None

time: 81.2 us -> 80.9 us (level)
  no operation moved by 1% of the time
where the time goes in v9:
time: 80.9 us; the launch traced here: 80.7 us
  Pallas kernels  80.7 us (100%)
    pallas_call x1, Pallas kernels, per_device(): pl.pallas_call(main_kernel, out_shape=[jax.ShapeDtypeStruct((3, order, L)...  73.4 us
    pallas_call x1, Pallas kernels, per_device(): pl.pallas_call(last_kernel, out_shape=jax.ShapeDtypeStruct(block, F32), i...  7.35 us

profile of v9, /device:TPU:1, one launch (start us, length us, event | category | flops | bytes accessed | tf_op | source)
XLA Modules:
  0.0 80.7 jit_solution(9603470108631764329)
XLA Ops:
  0.0 73.4 %lanczos.1 = (f32[3,48,128]{2,1,0:T(8,128)}, f32[48,48]{1,0:T(8,128)}, f32[48,16]{1,0:T(8,128)}, f32[16,16]{1,0:T(8,128)}, f32[16,128]{1,0:T(8,128)}) custom-call(f32[3,128]{1,0:T(4,128)} %pos_hbm.1, f32[3,16,128]{2,1,0:T(8,128)} %noise_hbm.1), custom_call_target="tpu_custom_call" | custom-call | tf_op jit(solution)/shard_map/lanczos/pallas_call | solution.py:584
  73.4 7.4 %finish.1 = f32[3,16,128]{2,1,0:T(8,128)} custom-call(f32[3,48,128]{2,1,0:T(8,128)} %get-tuple-element.10.vec_ref, f32[48,48]{1,0:T(8,128)} %get-tuple-element.11.tri_ref, f32[48,16]{1,0:T(8,128)} %get-tuple-element.12.mix_ref, f32[16,16]{1,0:T(8,128)} %get-tuple-element.13.low_ref, f32[16,128]{1,0:T(8,128)} %get-tuple-element.14.ztot_ref), custom_call_target="tpu_custom_call" | custom-call | tf_op jit(solution)/shard_map/finish/pallas_call | solution.py:633

commit v10 on v9

--- a/solution.py
+++ b/solution.py
@@ -526,13 +526,11 @@
     for c in range(3):
         q1, q2, wv = vec_ref[c, 0:16], vec_ref[c, 16:32], vec_ref[c, 32:48]
         vec_ref[c, 32:48] = mm(inv2, wv - mm(fat, q1) - mm(fbt, q2))
-    wide_recv(2, zb)
-    ztot_ref[...] = all_of(zb, NW)
 
     for phase, buffer in enumerate([cpos, xg0, xg1, xg2]):
         for p in (HALF[1:] if phase == 3 else range(1, NW)):
             block_copy(phase, buffer, p).wait_send()
-    for phase, buffer in enumerate([gb1, gb2, zb]):
+    for phase, buffer in enumerate([gb1, gb2]):
         wide_sent(phase, buffer)
     for phase, buffer in enumerate([ga1, ga2, za]):
         narrow_sent(phase, buffer)
@@ -541,6 +539,9 @@
         row_copy(1, pb1.at[q], rb1, q, True).wait_send()
         row_copy(2, pb2.at[q], rb2, q, True).wait_send()
         row_copy(3, xr.at[OWN], xr, q, False).wait_send()
+    wide_recv(2, zb)
+    ztot_ref[...] = all_of(zb, NW)
+    wide_sent(2, zb)
 
 
 def last_kernel(vec_ref, tri_ref, mix_ref, low_ref, ztot_ref, out_ref, y_ref, z_ref):

time: 80.9 us -> 80.6 us (level)
  no operation moved by 1% of the time
where the time goes in v10:
time: 80.6 us; the launch traced here: 80.4 us
  Pallas kernels  80.4 us (100%)
    pallas_call x1, Pallas kernels, per_device(): pl.pallas_call(main_kernel, out_shape=[jax.ShapeDtypeStruct((3, order, L)...  73 us
    pallas_call x1, Pallas kernels, per_device(): pl.pallas_call(last_kernel, out_shape=jax.ShapeDtypeStruct(block, F32), i...  7.35 us

profile of v10, /device:TPU:1, one launch (start us, length us, event | category | flops | bytes accessed | tf_op | source)
XLA Modules:
  0.0 80.4 jit_solution(4179008454787691867)
XLA Ops:
  0.0 73.0 %lanczos.1 = (f32[3,48,128]{2,1,0:T(8,128)}, f32[48,48]{1,0:T(8,128)}, f32[48,16]{1,0:T(8,128)}, f32[16,16]{1,0:T(8,128)}, f32[16,128]{1,0:T(8,128)}) custom-call(f32[3,128]{1,0:T(4,128)} %pos_hbm.1, f32[3,16,128]{2,1,0:T(8,128)} %noise_hbm.1), custom_call_target="tpu_custom_call" | custom-call | tf_op jit(solution)/shard_map/lanczos/pallas_call | solution.py:585
  73.0 7.4 %finish.1 = f32[3,16,128]{2,1,0:T(8,128)} custom-call(f32[3,48,128]{2,1,0:T(8,128)} %get-tuple-element.10.vec_ref, f32[48,48]{1,0:T(8,128)} %get-tuple-element.11.tri_ref, f32[48,16]{1,0:T(8,128)} %get-tuple-element.12.mix_ref, f32[16,16]{1,0:T(8,128)} %get-tuple-element.13.low_ref, f32[16,128]{1,0:T(8,128)} %get-tuple-element.14.ztot_ref), custom_call_target="tpu_custom_call" | custom-call | tf_op jit(solution)/shard_map/finish/pallas_call | solution.py:634
